TPU v7x, 128 devices: a whole 4x4x4 slice. The times are simulated.
128 devices in a mesh: vocab: 32 (over y, x, core), dp: 4 (over z).
Axes of the slice: x: 4, y: 4, z: 4, core: 2. Of those that a mesh axis runs over, the one named last changes fastest.
Arguments:
- token_ids: int32 [131072], P(('vocab', 'dp')), may hold values from 0 to 1048575, as said below
- counts: int32 [128], P(('vocab', 'dp')), may hold values from 256 to 1024, as said below
- table: bfloat16 [1048576, 128], P(('vocab', 'dp')), may hold values from -6 to 6
- projection: bfloat16 [128, 4096], replicated, may hold values from -0.5 to 0.5
- cotangent: bfloat16 [131072, 4096], P(('vocab', 'dp')), may hold values from -4 to 4
Outputs:
- hidden: bfloat16 [131072, 4096], P(('vocab', 'dp'))
- grad_projection: float32 [128, 4096], replicated
- grad_table: float32 [1048576, 128], P(('vocab', 'dp'))
Inputs may be any that keep to these rules, and one draw needn't show every extreme that they name: `token_ids`: on each device at most 16 tokens have ids in the rows of any one device, and in every draw one device's rows receive exactly 16 tokens from every device; which rows are frequent is drawn from the seed. `counts`: in every draw some device has all 1024 tokens live.
All inputs are finite; a program needn't handle non-finite values.
Results may differ from a plain program's by a relative error of at most 0.0029.
Values may be sent and summed in bfloat16 or wider, within the bound.
No kernel may reach another device: no remote copies, remote signals or barrier semaphores. Data moves between devices by JAX's collectives and lax.ppermute only.
A program may use at most 128 MiB of HBM per device.

v0:
```python
import math

import jax
import jax.numpy as jnp
from jax import lax
from jax.sharding import Mesh
from jax.sharding import PartitionSpec as P

VOCAB_DP = ("vocab_0", "vocab_1", "vocab_2", "dp")
VOCAB = ("vocab_0", "vocab_1", "vocab_2")


def rows_for(lines, length):
    spare = -lines.shape[0] % length
    if not spare:
        return lines
    return jnp.concatenate([lines, jnp.zeros((spare, *lines.shape[1:]), lines.dtype)])


def sent_to_all(value, axis):
    length = lax.axis_size(axis)
    return lax.all_to_all(
        jnp.broadcast_to(value[None], (length, *value.shape)), axis, 0, 0, tiled=True
    )


def joined_along(parts, dim):
    parts = jnp.moveaxis(parts, 0, dim)
    lengths = parts.shape
    return parts.reshape(*lengths[:dim], lengths[dim] * lengths[dim + 1], *lengths[dim + 2 :])


def whole_of(value, axes, dim):
    far, near = axes
    parts = sent_to_all(sent_to_all(value, far), near)
    return joined_along(parts.swapaxes(0, 1).reshape(-1, *value.shape), dim)


def in_blocks(value, dim, length):
    before, after = (value.shape[:dim], value.shape[dim + 1 :])
    return jnp.moveaxis(value.reshape(*before, length, -1, *after), dim, 0)


def sum_at_owner(value, axis, dim):
    parts = in_blocks(value, dim, lax.axis_size(axis))
    arrived = lax.all_to_all(parts, axis, split_axis=0, concat_axis=0, tiled=True)
    return arrived.sum(axis=0)


def summed_rows(value, axes, dim):
    far, near = axes
    parts = in_blocks(value, dim, lax.axis_size(far))
    nearer = sum_at_owner(parts, near, dim + 1)
    arrived = lax.all_to_all(nearer, far, split_axis=0, concat_axis=0, tiled=True)
    return arrived.sum(axis=0)


def sum_by_parts(value, axes):
    lines = value.reshape(-1, value.shape[-1])
    padded = rows_for(lines, lax.axis_size(axes[0]) * lax.axis_size(axes[1]))
    whole = whole_of(summed_rows(padded, axes, 0), axes, 0)
    return lax.slice_in_dim(whole, 0, len(lines)).reshape(value.shape)


def move_ids(requests):
    return lax.all_to_all(requests, VOCAB_DP, split_axis=0, concat_axis=0, tiled=True)


def move_rows(blocks):
    return lax.all_to_all(blocks, VOCAB_DP, split_axis=0, concat_axis=0, tiled=True)


def sum_projection(terms, scaling):
    return sum_by_parts(terms, (("vocab_0", "vocab_1"), ("vocab_2", "dp"))) * scaling


def body(token_ids, counts, table, projection, cotangent):
    tokens_here = token_ids.shape[0]
    held_rows = table.shape[0]
    width = table.shape[1]
    n_vocab = lax.axis_size(VOCAB)
    n_data = lax.axis_size("dp")
    devices_all = n_vocab * n_data
    capacity = max(4, 2 * tokens_here // devices_all)
    owner = token_ids // held_rows
    local_row = token_ids - owner * held_rows
    owner_hits = (owner[:, None] == jnp.arange(devices_all, dtype=jnp.int32)[None, :]).astype(
        jnp.int32
    )
    rank = jnp.sum(jnp.cumsum(owner_hits, axis=0) * owner_hits, axis=1) - 1
    slot_index = owner * capacity + rank
    requests = jnp.full((devices_all * capacity,), -1, jnp.int32).at[slot_index].set(local_row)
    received = move_ids(requests.reshape(devices_all, capacity)).reshape(-1)
    valid = received >= 0
    safe_rows = jnp.maximum(received, 0)
    picked = jnp.where(valid[:, None], table[safe_rows], jnp.zeros((1, width), table.dtype))
    returned = move_rows(picked.reshape(devices_all, capacity, width)).reshape(-1, width)
    embedded = returned[slot_index]
    live = jnp.arange(tokens_here, dtype=jnp.int32) < counts[0]
    product = jnp.dot(embedded, projection, preferred_element_type=jnp.float32)
    hidden = jnp.where(live[:, None], product, 0.0).astype(jnp.bfloat16)
    masked = jnp.where(live[:, None], cotangent, jnp.zeros_like(cotangent))
    token_grad = lax.dot_general(
        masked, projection, (((1,), (1,)), ((), ())), preferred_element_type=jnp.float32
    ).astype(jnp.bfloat16)
    outgoing = (
        jnp.zeros((devices_all * capacity, width), jnp.bfloat16).at[slot_index].set(token_grad)
    )
    incoming = move_rows(outgoing.reshape(devices_all, capacity, width)).reshape(-1, width)
    grad_table = jax.ops.segment_sum(
        incoming.astype(jnp.float32), safe_rows, num_segments=held_rows
    )
    terms = lax.dot_general(
        embedded, masked, (((0,), (0,)), ((), ())), preferred_element_type=jnp.float32
    )
    scaling = 1.0 / math.sqrt(tokens_here * devices_all)
    grad_projection = sum_projection(terms, scaling)
    return (hidden, grad_projection, grad_table)


def solution(mesh):
    finer = Mesh(
        mesh.devices.reshape(4, 4, 2, mesh.shape["dp"]), ("vocab_0", "vocab_1", "vocab_2", "dp")
    )
    in_specs = (P(VOCAB_DP), P(VOCAB_DP), P(VOCAB_DP, None), P(), P(VOCAB_DP, None))
    out_specs = (P(VOCAB_DP, None), P(), P(VOCAB_DP, None))
    return jax.shard_map(body, mesh=finer, in_specs=in_specs, out_specs=out_specs, check_vma=False)
```

profile of v0, /device:TPU:1, one launch (start us, length us, event | category | flops | bytes accessed | tf_op | source)
XLA Modules:
  0.0 180.6 jit_solution(10058417289933348476)
XLA Ops:
  3.1 4.3 %scatter_custom_fusion = s32[2048]{0:T(1024)S(1)} fusion(s32[1024]{0:T(1024)S(1)} %get-tuple-element.4, s32[1024]{0:T(1024)S(1)} %get-tuple-element.5, s32[]{:T(128)} %constant.13.clone.1), kind=kCustom, calls=%fused_computation.40 | custom fusion | bytes 8196 | tf_op jit(solution)/shard_map/scatter | solution.py:92
  7.5 21.0 %all_to_all.39 = s32[128,1,16]{2,1,0:T(1,128)S(1)} all-to-all(s32[128,1,16]{2,1,0:T(1,128)S(1)} %bitcast.45), channel_id=1, replica_groups=mesh['vocab_0'=4,'vocab_1'=4,'vocab_2'=2,'dp'=4] {'vocab_0','vocab_1','v..., dimensions={0} | all-to-all | bytes 16384 | tf_op jit(solution)/shard_map/all_to_all | solution.py:66
  28.8 6.2 %gather_fusion = bf16[2048,128]{1,0:T(8,128)(2,1)S(1)} fusion(bf16[8192,128]{1,0:T(8,128)(2,1)S(1)} %copy-done, s32[2048]{0:T(1024)S(1)} %broadcast_clamp_fusion), kind=kCustom, calls=%fused_computation | custom fusion | bytes 1056768 | tf_op jit(solution)/shard_map/gather | solution.py:96
  35.0 1.1 broadcast_select_fusion.5
  36.2 4.3 %all-to-all-start.1 = ((bf16[128,16,128]{2,1,0:T(8,128)(2,1)}), bf16[128,16,128]{2,1,0:T(8,128)(2,1)S(1)}, u32[]{:S(2)}, u32[]{:S(2)}) async-start(bf16[128,16,128]{2,1,0:T(8,128)(2,1)} %broadcast_select_fusion.5), calls=%async_computation.1 | async-start | bytes 1048576 | tf_op jit(solution)/shard_map/all_to_all | solution.py:70
  41.2 13.1 %all-to-all-done.1 = bf16[128,16,128]{2,1,0:T(8,128)(2,1)S(1)} async-done(((bf16[128,16,128]{2,1,0:T(8,128)(2,1)}), bf16[128,16,128]{2,1,0:T(8,128)(2,1)S(1)}, u32[]{:S(2)}, u32[]{:S(2)}) %all-to-all-start.1) | async-done | bytes 524320 | tf_op jit(solution)/shard_map/all_to_all | solution.py:70
  54.3 3.2 %gather_fusion.1 = bf16[1024,128]{1,0:T(8,128)(2,1)S(1)} fusion(bf16[2048,128]{1,0:T(8,128)(2,1)S(1)} %bitcast.40, s32[1024]{0:T(1024)S(1)} %get-tuple-element.3), kind=kCustom, calls=%fused_computation.1 | custom fusion | bytes 528384 | tf_op jit(solution)/shard_map/gather | solution.py:98
  57.5 4.7 %convolution_bitcast_fusion = f32[16,8,1,4096]{3,1,0,2:T(8,128)S(1)} fusion(bf16[1024,128]{1,0:T(8,128)(2,1)S(1)} %gather_fusion.1, bf16[1024,4096]{1,0:T(8,128)(2,1)} %param.9, pred[1024]{0:T(1024)(128)(4,1)S(1)} %iota_compare_fusion.3), kind=kOutput, calls=%fused_computation.7 | convolution fusion | flops 1077936128 | bytes 10748928 | tf_op jit(solution)/shard_map/dot_general | solution.py:113
  62.2 1.2 copy.29
  63.5 29.7 %all_to_all.40 = f32[8,16,1,4096]{3,1,2,0:T(8,128)} all-to-all(f32[8,16,1,4096]{3,1,2,0:T(8,128)S(1)} %bitcast.41), channel_id=1, replica_groups=mesh['vocab_0'=4,'vocab_1'=4,'vocab_2'=2,'dp'=4] {'vocab_2','dp'}, dimensions={0} | all-to-all | bytes 4194304 | tf_op jit(solution)/shard_map/all_to_all | solution.py:46
  93.2 1.7 reduce_sum.30
  95.2 11.3 %all_to_all.41 = f32[16,1,4096]{2,1,0:T(1,128)S(1)} all-to-all(f32[16,1,4096]{2,1,0:T(1,128)S(1)} %reduce_sum.31), channel_id=1, replica_groups=mesh['vocab_0'=4,'vocab_1'=4,'vocab_2'=2,'dp'=4] {'vocab_0','vocab_1'}, dimensions={0} | all-to-all | bytes 524288 | tf_op jit(solution)/shard_map/all_to_all | solution.py:54
  106.6 0.9 broadcast_in_dim.80
  107.5 3.5 %all-to-all-start.4 = ((f32[16,1,4096]{2,1,0:T(1,128)}), f32[16,1,4096]{2,1,0:T(1,128)S(1)}, u32[]{:S(2)}, u32[]{:S(2)}) async-start(f32[16,1,4096]{2,1,0:T(1,128)} %broadcast_in_dim.80), calls=%async_computation.4 | async-start | bytes 524288 | tf_op jit(solution)/shard_map/all_to_all | solution.py:22
  111.1 6.0 %fusion.4 = bf16[1024,128]{1,0:T(8,128)(2,1)S(1)} fusion(bf16[128,4096]{1,0:T(8,128)(2,1)} %param.8, bf16[1024,4096]{1,0:T(8,128)(2,1)} %param.9, pred[1024]{0:T(1024)(128)(4,1)S(1)} %iota_compare_fusion.3), kind=kOutput, calls=%fused_computation.14 | convolution fusion | flops 1078067200 | bytes 9700352 | tf_op jit(solution)/shard_map/dot_general | solution.py:103
  117.1 4.0 %scatter_custom_fusion.1 = bf16[2048,128]{1,0:T(8,128)(2,1)} fusion(s32[1024]{0:T(1024)S(1)} %get-tuple-element.4, bf16[1024,128]{1,0:T(8,128)(2,1)S(1)} %fusion.4, bf16[]{:T(256)} %constant.40.clone.1), kind=kCustom, calls=%fused_computation.24 | custom fusion | bytes 524290 | tf_op jit(solution)/shard_map/scatter | solution.py:107
  121.1 9.0 %all-to-all-start.6 = ((bf16[128,16,128]{2,1,0:T(8,128)(2,1)}), bf16[128,16,128]{2,1,0:T(8,128)(2,1)S(1)}, u32[]{:S(2)}, u32[]{:S(2)}) async-start(bf16[128,16,128]{2,1,0:T(8,128)(2,1)} %bitcast.13), calls=%async_computation.6 | async-start | bytes 1048576 | tf_op jit(solution)/shard_map/all_to_all | solution.py:70
  130.3 13.6 %all-to-all-done.6 = bf16[128,16,128]{2,1,0:T(8,128)(2,1)S(1)} async-done(((bf16[128,16,128]{2,1,0:T(8,128)(2,1)}), bf16[128,16,128]{2,1,0:T(8,128)(2,1)S(1)}, u32[]{:S(2)}, u32[]{:S(2)}) %all-to-all-start.6) | async-done | bytes 524320 | tf_op jit(solution)/shard_map/all_to_all | solution.py:70
  143.9 1.5 broadcast_in_dim.82
  145.4 4.6 %all-to-all-start.5 = ((f32[8,16,1,4096]{3,1,2,0:T(8,128)}), f32[8,16,1,4096]{3,1,2,0:T(8,128)}, u32[]{:S(2)}, u32[]{:S(2)}) async-start(f32[8,16,1,4096]{3,1,2,0:T(8,128)} %broadcast_in_dim.82), calls=%async_computation.5 | async-start | bytes 4194304 | tf_op jit(solution)/shard_map/all_to_all | solution.py:22
  150.0 13.7 %scatter_custom_fusion.2 = f32[8192,128]{1,0:T(8,128)} fusion(s32[2048]{0:T(1024)S(1)} %reshape.90, f32[]{:T(128)} %constant.41.clone.1, bf16[2048,128]{1,0:T(8,128)(2,1)S(1)} %bitcast.42), kind=kCustom, calls=%fused_computation.12 | custom fusion | flops 524288 | bytes 4718596 | tf_op jit(solution)/shard_map/scatter-add | solution.py:110
  163.8 5.9 %select_convert_fusion = bf16[1024,4096]{1,0:T(8,128)(2,1)} fusion(bf16[1024,128]{1,0:T(8,128)(2,1)S(1)} %gather_fusion.1, bf16[128,4096]{1,0:T(8,128)(2,1)} %param.8, pred[1024]{0:T(1024)(128)(4,1)S(1)} %iota_compare_fusion.3), kind=kOutput, calls=%fused_computation.5 | convolution fusion | flops 1082130432 | bytes 9700352 | tf_op jit(solution)/shard_map/dot_general | solution.py:100
  169.6 6.7 %all-to-all-done.5 = f32[8,16,1,4096]{3,1,2,0:T(8,128)} async-done(((f32[8,16,1,4096]{3,1,2,0:T(8,128)}), f32[8,16,1,4096]{3,1,2,0:T(8,128)}, u32[]{:S(2)}, u32[]{:S(2)}) %all-to-all-start.5) | async-done | bytes 2097184 | tf_op jit(solution)/shard_map/all_to_all | solution.py:22
  176.3 4.3 %fusion.1 = f32[128,4096]{1,0:T(8,128)} fusion(f32[8,16,1,4096]{3,1,2,0:T(8,128)} %all-to-all-done.5), kind=kLoop, calls=%fused_computation.10 | loop fusion | flops 524288 | bytes 4194304 | tf_op jit(solution)/shard_map/mul | solution.py:74
  (25 shorter events, 3.5 us)
Async XLA Ops:
  0.6 28.2 %copy-start = (bf16[8192,128]{1,0:T(8,128)(2,1)S(1)}, bf16[8192,128]{1,0:T(8,128)(2,1)}, u32[]{:S(2)}) copy-start(bf16[8192,128]{1,0:T(8,128)(2,1)} %param.7) | copy-start | bytes 6291460
  36.2 18.1 %all-to-all-start.1 = ((bf16[128,16,128]{2,1,0:T(8,128)(2,1)}), bf16[128,16,128]{2,1,0:T(8,128)(2,1)S(1)}, u32[]{:S(2)}, u32[]{:S(2)}) async-start(bf16[128,16,128]{2,1,0:T(8,128)(2,1)} %broadcast_select_fusion.5), calls=%async_computation.1 | async-start | bytes 1048576 | tf_op jit(solution)/shard_map/all_to_all | solution.py:70
  107.5 13.5 %all-to-all-start.4 = ((f32[16,1,4096]{2,1,0:T(1,128)}), f32[16,1,4096]{2,1,0:T(1,128)S(1)}, u32[]{:S(2)}, u32[]{:S(2)}) async-start(f32[16,1,4096]{2,1,0:T(1,128)} %broadcast_in_dim.80), calls=%async_computation.4 | async-start | bytes 524288 | tf_op jit(solution)/shard_map/all_to_all | solution.py:22
  121.1 22.8 %all-to-all-start.6 = ((bf16[128,16,128]{2,1,0:T(8,128)(2,1)}), bf16[128,16,128]{2,1,0:T(8,128)(2,1)S(1)}, u32[]{:S(2)}, u32[]{:S(2)}) async-start(bf16[128,16,128]{2,1,0:T(8,128)(2,1)} %bitcast.13), calls=%async_computation.6 | async-start | bytes 1048576 | tf_op jit(solution)/shard_map/all_to_all | solution.py:70
  145.4 30.9 %all-to-all-start.5 = ((f32[8,16,1,4096]{3,1,2,0:T(8,128)}), f32[8,16,1,4096]{3,1,2,0:T(8,128)}, u32[]{:S(2)}, u32[]{:S(2)}) async-start(f32[8,16,1,4096]{3,1,2,0:T(8,128)} %broadcast_in_dim.82), calls=%async_computation.5 | async-start | bytes 4194304 | tf_op jit(solution)/shard_map/all_to_all | solution.py:22
where the time goes:
time: 181 us
  blocking collectives  62 us (34%)
  waiting for transfers between devices  33.4 us (18%)
  other arithmetic  23.2 us (13%)
  local copies, waits for them, and re-layouts  22.4 us (12%)
  starting transfers between devices  21.5 us (12%)
  matrix products  16.6 us (9%)
    all_to_all x1, blocking collectives, sum_at_owner(): lax.all_to_all(parts, axis, split_axis=0, concat_axis=0, tiled=True)  29.7 us
    all_to_all x2, waiting for transfers between devices, move_rows(): lax.all_to_all(blocks, VOCAB_DP, split_axis=0, concat_axis=0, tiled=True)  26.7 us
    all_to_all x1, blocking collectives, move_ids(): lax.all_to_all(requests, VOCAB_DP, split_axis=0, concat_axis=0, tiled=True)  21 us
    scatter-add x1, other arithmetic, body(): jax.ops.segment_sum(incoming.astype(jnp.float32), safe_rows, num_segments...  13.7 us
    all_to_all x2, starting transfers between devices, move_rows(): lax.all_to_all(blocks, VOCAB_DP, split_axis=0, concat_axis=0, tiled=True)  13.3 us
    all_to_all x1, blocking collectives, summed_rows(): lax.all_to_all(nearer, far, split_axis=0, concat_axis=0, tiled=True)  11.3 us
    all_to_all x2, starting transfers between devices, sent_to_all(): lax.all_to_all(jnp.broadcast_to(value[None], (length, *value.shape)), axi...  8.17 us
    all_to_all x2, waiting for transfers between devices, sent_to_all(): lax.all_to_all(jnp.broadcast_to(value[None], (length, *value.shape)), axi...  6.7 us
  transfers between devices with their start and end apart: 4, of which 3 were waited for; matrix products, arithmetic and copies ran while one was open for 16% of the time, Pallas kernels for 0%

commit v1 on v0

v1 whole, which is shorter than its diff:
```python
import functools
import math

import jax
import jax.numpy as jnp
from jax import lax
from jax.experimental import pallas as pl
from jax.experimental.pallas import tpu as pltpu
from jax.sharding import Mesh
from jax.sharding import PartitionSpec as P


ALL = ("vocab_0", "vocab_1", "vocab_2", "dp")
CHIPS = ("vocab_0", "vocab_1", "dp")
CORE = "vocab_2"
SWAP = ((0, 1), (1, 0))
LANES = 128
BF16 = jnp.bfloat16
F32 = jnp.float32
VMEM = pl.BlockSpec(memory_space=pltpu.VMEM)
SMEM = pl.BlockSpec(memory_space=pltpu.SMEM)
HBM = pl.BlockSpec(memory_space=pltpu.HBM)


def in_hbm(x):
    return pltpu.with_memory_space_constraint(x, pltpu.HBM)


def in_vmem(x):
    return pltpu.with_memory_space_constraint(x, pltpu.VMEM)


def params(mib):
    return pltpu.CompilerParams(vmem_limit_bytes=mib << 20)


def cost(flops, nbytes):
    return pl.CostEstimate(flops=flops, bytes_accessed=nbytes, transcendentals=0)


def dot(a, b, dims=((1,), (0,))):
    return lax.dot_general(a, b, (dims, ((), ())), preferred_element_type=F32)


def one_hot(hit):
    return jnp.where(hit, 1.0, 0.0).astype(BF16)


def exchange(blocks, axes):
    return lax.all_to_all(blocks, axes, split_axis=0, concat_axis=0, tiled=True)


def front_kernel(
    shift, capacity, count_ref, ids_ref, proj_hbm, cot_hbm, slot_ref, out_ref, cot, proj, across, grads, sems
):
    tokens, _ = cot.shape
    steps = slot_ref.shape[0]
    block = tokens // steps
    proj_copy = pltpu.make_async_copy(proj_hbm, proj, sems.at[steps])
    proj_copy.start()
    copies = []
    for i in range(steps):
        rows = pl.ds(i * block, block)
        copies.append(pltpu.make_async_copy(cot_hbm.at[rows, :], cot.at[rows, :], sems.at[i]))
        copies[-1].start()

    ids = ids_ref[...]
    owner = lax.shift_right_logical(ids, shift)
    row = ids & ((1 << shift) - 1)
    chunks, lanes = ids.shape
    n = out_ref.shape[0] // (capacity + 2)
    holder = lax.broadcasted_iota(jnp.int32, (n, lanes), 0)
    before = one_hot(
        lax.broadcasted_iota(jnp.int32, (lanes, lanes), 0)
        < lax.broadcasted_iota(jnp.int32, (lanes, lanes), 1)
    )
    place = lax.broadcasted_iota(jnp.int32, (LANES, lanes), 0)
    seen = jnp.zeros((n, 1), F32)
    high = jnp.zeros((n, LANES), F32)
    low = jnp.zeros((n, LANES), F32)
    targets = []
    for k in range(chunks):
        own = owner[k : k + 1, :]
        hit = holder == own
        hits = one_hot(hit)
        earlier = dot(hits, before) + seen
        rank = jnp.sum(jnp.where(hit, earlier, 0.0), axis=0, keepdims=True).astype(jnp.int32)
        seen = seen + jnp.sum(jnp.where(hit, 1.0, 0.0), axis=1, keepdims=True)
        per = block // lanes
        slot_ref[k // per, :, (k % per) * lanes : (k % per + 1) * lanes] = own * capacity + rank
        targets.append(own * (capacity + 2) + rank)
        mine = place == rank
        line = row[k : k + 1, :]
        upper = lax.shift_right_logical(line, 7).astype(F32)
        lower = (line & 127).astype(F32)
        high = high + dot(hits, jnp.where(mine, upper, 0.0).astype(BF16), ((1,), (1,)))
        low = low + dot(hits, jnp.where(mine, lower, 0.0).astype(BF16), ((1,), (1,)))
    last = lax.broadcasted_iota(jnp.int32, (1, n), 1) * (capacity + 2) + capacity
    targets += [last, last + 1]
    grads[tokens : tokens + n, :] = high.astype(BF16)
    grads[tokens + n : tokens + 2 * n, :] = low.astype(BF16)

    proj_copy.wait()
    across[...] = proj[...].T
    for i in range(steps):
        copies[i].wait()
        rows = slice(i * block, (i + 1) * block)
        grad = dot(cot[rows, :], across[...])
        token = lax.broadcasted_iota(jnp.int32, grad.shape, 0) + i * block
        grads[rows, :] = jnp.where(token < count_ref[0], grad, 0.0).astype(BF16)

    step = 256
    line = lax.broadcasted_iota(jnp.int32, (step, lanes), 0)
    for c in range(out_ref.shape[0] // step):
        total = jnp.zeros((step, out_ref.shape[1]), F32)
        for k in range(0, len(targets), 2):
            left = one_hot(line == targets[k] - c * step)
            right = one_hot(line == targets[k + 1] - c * step)
            total += dot(
                jnp.concatenate([left, right], axis=1), grads[k * lanes : (k + 2) * lanes, :]
            )
        out_ref[c * step : (c + 1) * step, :] = total.astype(BF16)


def front(counts, token_ids, projection, cotangent, held_rows, n, capacity, block):
    tokens, hidden = cotangent.shape
    width = projection.shape[0]
    shift = held_rows.bit_length() - 1
    assert held_rows == 1 << shift and shift <= 15 and n == width == LANES
    rows = n * (capacity + 2)
    return pl.pallas_call(
        functools.partial(front_kernel, shift, capacity),
        out_shape=(
            jax.ShapeDtypeStruct((tokens // block, 1, block), jnp.int32),
            jax.ShapeDtypeStruct((rows, width), BF16),
        ),
        in_specs=[SMEM, VMEM, HBM, HBM],
        out_specs=(VMEM, VMEM),
        scratch_shapes=[
            pltpu.VMEM((tokens, hidden), BF16),
            pltpu.VMEM((width, hidden), BF16),
            pltpu.VMEM((hidden, width), BF16),
            pltpu.VMEM((tokens + 2 * n, width), BF16),
            pltpu.SemaphoreType.DMA((tokens // block + 1,)),
        ],
        compiler_params=params(24),
        cost_estimate=cost(3 << 29, 10 << 20),
        name="front",
    )(counts, token_ids.reshape(tokens // LANES, LANES), in_hbm(projection), in_hbm(cotangent))


def hold_kernel(table_hbm, out_ref, sem):
    copy = pltpu.make_async_copy(table_hbm, out_ref, sem)
    copy.start()
    copy.wait()


def held_table(table):
    return pl.pallas_call(
        hold_kernel,
        out_shape=pltpu.VMEM(table.shape, table.dtype),
        in_specs=[HBM],
        out_specs=VMEM,
        scratch_shapes=[pltpu.SemaphoreType.DMA(())],
        compiler_params=params(4),
        cost_estimate=cost(1 << 22, 6 << 20),
        name="held_table",
    )(in_hbm(table))


def pick_kernel(capacity, arrived_ref, table_ref, out_ref, index_ref, wide, index, table, stage, sem):
    wide[...] = arrived_ref[...].astype(F32)
    n = index_ref.shape[1]
    high = wide[pl.ds(capacity, n, stride=capacity + 2), :]
    low = wide[pl.ds(capacity + 1, n, stride=capacity + 2), :]
    rows = (high * 128.0 + low).T
    index_ref[...] = rows[:capacity, :].astype(jnp.int32)
    copy = pltpu.make_async_copy(index_ref, index, sem)
    copy.start()
    step = 256

    @pl.loop(0, table_ref.shape[0] // step)
    def _(c):
        part = pl.ds(pl.multiple_of(c * step, step), step)
        table[part, :] = table_ref[part, :].astype(F32)

    copy.wait()
    unroll = 4

    @pl.loop(0, n // unroll)
    def _(q):
        for k in range(unroll):
            p = q * unroll + k
            for r in range(capacity):
                stage[pl.ds(p * capacity + r, 1), :] = table[pl.ds(index[r, p], 1), :]

    out_ref[...] = stage[...].astype(BF16)


def picked_rows(arrived, table, n, capacity):
    rows, width = arrived.shape
    slots = n * capacity
    return pl.pallas_call(
        functools.partial(pick_kernel, capacity),
        out_shape=(
            jax.ShapeDtypeStruct((slots, width), BF16),
            jax.ShapeDtypeStruct((capacity, n), jnp.int32),
        ),
        in_specs=[VMEM, VMEM],
        out_specs=(VMEM, VMEM),
        scratch_shapes=[
            pltpu.VMEM((rows, width), F32),
            pltpu.SMEM((capacity, n), jnp.int32),
            pltpu.VMEM(table.shape, F32),
            pltpu.VMEM((slots, width), F32),
            pltpu.SemaphoreType.DMA(()),
        ],
        compiler_params=params(12),
        cost_estimate=cost(1 << 26, 3 << 20),
        name="picked_rows",
    )(arrived, table)


def rows_sum_kernel(capacity, index_ref, grads_ref, out_ref, wide, first, second, third):
    sums = (out_ref, first, second, third)
    step = 256

    @pl.loop(0, out_ref.shape[0] // step)
    def _(c):
        rows = pl.ds(pl.multiple_of(c * step, step), step)
        for total in sums:
            total[rows, :] = jnp.zeros((step, out_ref.shape[1]), F32)

    wide[...] = grads_ref[...].astype(F32)
    n = index_ref.shape[1]
    quarter = n // len(sums)

    @pl.loop(0, quarter)
    def _(q):
        for r in range(capacity):
            for s, total in enumerate(sums):
                p = q + s * quarter
                row = pl.ds(index_ref[r, p], 1)
                total[row, :] += wide[pl.ds(p * (capacity + 2) + r, 1), :]

    @pl.loop(0, out_ref.shape[0] // step)
    def _(c):
        rows = pl.ds(pl.multiple_of(c * step, step), step)
        out_ref[rows, :] = (out_ref[rows, :] + first[rows, :]) + (second[rows, :] + third[rows, :])


def rows_sum(index, arrived, held_rows, capacity):
    rows, width = arrived.shape
    return pl.pallas_call(
        functools.partial(rows_sum_kernel, capacity),
        out_shape=jax.ShapeDtypeStruct((held_rows, width), F32),
        in_specs=[SMEM, VMEM],
        out_specs=VMEM,
        scratch_shapes=[
            pltpu.VMEM((rows, width), F32),
            pltpu.VMEM((held_rows, width), F32),
            pltpu.VMEM((held_rows, width), F32),
            pltpu.VMEM((held_rows, width), F32),
        ],
        compiler_params=params(24),
        cost_estimate=cost(1 << 28, 6 << 20),
        name="rows_sum",
    )(index, arrived)


def cot_copies(half_ref, cot_hbm, cot, sems):
    tokens, wide = cot.shape
    steps = sems.shape[0]
    block = tokens // steps
    columns = pl.ds(pl.multiple_of(half_ref[0] * wide, wide), wide)
    copies = []
    for i in range(steps):
        rows = pl.ds(i * block, block)
        copies.append(
            pltpu.make_async_copy(cot_hbm.at[rows, columns], cot.at[rows, :], sems.at[i])
        )
        copies[-1].start()
    return copies


def half_product(emb_ref, cot, copies, out_ref):
    block = 512
    for copy in copies:
        copy.wait()
    for i in range(out_ref.shape[1] // block):
        columns = slice(i * block, (i + 1) * block)
        out_ref[:, columns] = dot(emb_ref[...], cot[:, columns])


def terms_kernel(half_ref, emb_ref, cot_hbm, out_ref, cot, sems):
    copies = cot_copies(half_ref, cot_hbm, cot, sems)
    half_product(emb_ref, cot, copies, out_ref)


def first_terms_kernel(
    half_ref, count_ref, slot_ref, rows_ref, cot_hbm, emb_ref, out_ref, cot, sems
):
    copies = cot_copies(half_ref, cot_hbm, cot, sems)
    across = rows_ref[...].T
    chunks, _, block = slot_ref.shape
    step = 256
    for k in range(chunks):
        slot = slot_ref[k]
        total = jnp.zeros((across.shape[0], block), F32)
        line = lax.broadcasted_iota(jnp.int32, (step, block), 0)
        for c in range(across.shape[1] // step):
            total += dot(across[:, c * step : (c + 1) * step], one_hot(line + c * step == slot))
        token = lax.broadcasted_iota(jnp.int32, total.shape, 1) + k * block
        total = jnp.where(token < count_ref[0], total, 0.0)
        emb_ref[:, k * block : (k + 1) * block] = total.astype(BF16)
    half_product(emb_ref, cot, copies, out_ref)


def first_terms(half, counts, slots, returned, cotangent):
    tokens, hidden = cotangent.shape
    width = returned.shape[1]
    return pl.pallas_call(
        first_terms_kernel,
        in_specs=[SMEM, SMEM, VMEM, VMEM, HBM],
        out_specs=(VMEM, VMEM),
        scratch_shapes=[
            pltpu.VMEM((tokens, hidden // 2), BF16),
            pltpu.SemaphoreType.DMA((4,)),
        ],
        out_shape=(
            jax.ShapeDtypeStruct((width, tokens), BF16),
            jax.ShapeDtypeStruct((width, hidden // 2), F32),
        ),
        compiler_params=params(16),
        cost_estimate=cost(3 << 28, 6 << 20),
        name="first_terms",
    )(half, counts, slots, returned, in_hbm(cotangent))


def half_terms(half, embedded, cotangent):
    tokens, hidden = cotangent.shape
    width = embedded.shape[0]
    return pl.pallas_call(
        terms_kernel,
        in_specs=[SMEM, VMEM, HBM],
        out_specs=VMEM,
        scratch_shapes=[
            pltpu.VMEM((tokens, hidden // 2), BF16),
            pltpu.SemaphoreType.DMA((4,)),
        ],
        out_shape=jax.ShapeDtypeStruct((width, hidden // 2), F32),
        compiler_params=params(16),
        cost_estimate=cost(1 << 29, 5 << 20),
        name="half_terms",
    )(half, embedded, in_hbm(cotangent))


def parts_kernel(tiles, mine_ref, other_ref, out_ref):
    groups = mine_ref.shape[1] // (tiles * LANES)
    for g in range(mine_ref.shape[0] // 8):
        rows = slice(8 * g, 8 * g + 8)
        for j in range(groups):
            columns = slice(j * tiles * LANES, (j + 1) * tiles * LANES)
            total = mine_ref[rows, columns] + other_ref[rows, columns]
            block = [total[:, t * LANES : (t + 1) * LANES] for t in range(tiles)]
            out_ref[g * groups + j] = jnp.concatenate(block, axis=0).astype(BF16)


def chip_parts(mine, other, chips):
    rows, columns = mine.shape
    tiles = rows * columns // (8 * LANES * chips)
    return pl.pallas_call(
        functools.partial(parts_kernel, tiles),
        out_shape=jax.ShapeDtypeStruct((chips, 8 * tiles, LANES), BF16),
        in_specs=[VMEM, VMEM],
        out_specs=VMEM,
        compiler_params=params(8),
        cost_estimate=cost(1 << 24, 3 << 20),
        name="chip_parts",
    )(mine, other)


def total_kernel(parts_ref, out_ref):
    total = parts_ref[0].astype(F32)
    for p in range(1, parts_ref.shape[0]):
        total += parts_ref[p].astype(F32)
    total = total.astype(BF16)
    for p in range(out_ref.shape[0]):
        out_ref[p] = total


def chips_total(parts):
    return pl.pallas_call(
        total_kernel,
        out_shape=jax.ShapeDtypeStruct(parts.shape, BF16),
        in_specs=[VMEM],
        out_specs=VMEM,
        compiler_params=params(8),
        cost_estimate=cost(1 << 24, 1 << 20),
        name="chips_total",
    )(parts)


def result_kernel(tiles, scaling, core_ref, mine_ref, other_ref, out_ref):
    half = out_ref.shape[1] // 2
    groups = half // (tiles * LANES)
    for side in range(2):
        for source, core in ((mine_ref, side), (other_ref, 1 - side)):

            @pl.when(core_ref[0] == core)
            def _():
                for g in range(out_ref.shape[0] // 8):
                    for j in range(groups):
                        block = source[g * groups + j].astype(F32) * scaling
                        for t in range(tiles):
                            left = side * half + (j * tiles + t) * LANES
                            out_ref[8 * g : 8 * g + 8, left : left + LANES] = block[
                                8 * t : 8 * t + 8, :
                            ]


def result(core, mine, other, width, hidden, scaling):
    tiles = mine.shape[1] // 8
    return pl.pallas_call(
        functools.partial(result_kernel, tiles, scaling),
        out_shape=jax.ShapeDtypeStruct((width, hidden), F32),
        in_specs=[SMEM, VMEM, VMEM],
        out_specs=VMEM,
        compiler_params=params(8),
        cost_estimate=cost(1 << 24, 3 << 20),
        name="result",
    )(core, mine, other)


def hidden_kernel(emb_ref, proj_ref, out_ref):
    out_ref[...] = dot(emb_ref[...].T, proj_ref[...]).astype(BF16)


def hidden_rows(embedded, projection):
    width, tokens = embedded.shape
    hidden = projection.shape[1]
    block = 256
    return pl.pallas_call(
        hidden_kernel,
        grid=(tokens // block,),
        out_shape=jax.ShapeDtypeStruct((tokens, hidden), BF16),
        in_specs=[
            pl.BlockSpec((width, block), lambda i: (0, i)),
            pl.BlockSpec((width, hidden), lambda i: (0, 0)),
        ],
        out_specs=pl.BlockSpec((block, hidden), lambda i: (i, 0)),
        compiler_params=params(16),
        cost_estimate=cost(1 << 30, 9 << 20),
        name="hidden_rows",
    )(embedded, projection)


def body(token_ids, counts, table, projection, cotangent):
    tokens = token_ids.shape[0]
    held_rows, width = table.shape
    hidden_width = projection.shape[1]
    n = lax.axis_size(ALL)
    chips = lax.axis_size(CHIPS)
    capacity = 2 * tokens // n
    core = lax.axis_index(CORE).astype(jnp.int32).reshape(1)
    slots, outgoing = front(counts, token_ids, projection, cotangent, held_rows, n, capacity, 256)
    incoming = exchange(outgoing.reshape(n, -1, 2, width), ALL).reshape(-1, width)
    held = held_table(table)
    picked, index = picked_rows(incoming, in_vmem(held), n, capacity)
    returned = exchange(picked.reshape(n, capacity, width), ALL).reshape(-1, width)
    embedded, theirs = first_terms(1 - core, counts, slots, returned, cotangent)
    other = lax.ppermute(theirs, CORE, SWAP)
    mine = half_terms(core, embedded, cotangent)
    parts = chip_parts(mine, other, chips)
    arrived = exchange(parts, CHIPS)
    hidden = hidden_rows(embedded, projection)
    total = chips_total(arrived)
    whole = exchange(total, CHIPS)
    across = lax.ppermute(whole, CORE, SWAP)
    scaling = 1.0 / math.sqrt(tokens * n)
    grad_projection = result(core, whole, across, width, hidden_width, scaling)
    grad_table = rows_sum(index, incoming, held_rows, capacity)
    return (hidden, grad_projection, grad_table)


def solution(mesh):
    finer = Mesh(
        mesh.devices.reshape(4, 4, 2, mesh.shape["dp"]), ("vocab_0", "vocab_1", "vocab_2", "dp")
    )
    in_specs = (P(ALL), P(ALL), P(ALL, None), P(), P(ALL, None))
    out_specs = (P(ALL, None), P(), P(ALL, None))
    return jax.shard_map(body, mesh=finer, in_specs=in_specs, out_specs=out_specs, check_vma=False)
```

time: 181 us -> 117 us (0.65)
  Pallas kernels: 0 us -> 35.5 us
  blocking collectives: 62 us -> 33.4 us
  other arithmetic: 23.2 us -> 0 us
  local copies, waits for them, and re-layouts: 22.4 us -> 0.69 us
  matrix products: 16.6 us -> 0 us
  waiting for transfers between devices: 33.4 us -> 26.6 us
  starting transfers between devices: 21.5 us -> 19.1 us
    pallas_call x0 -> x10, Pallas kernels: none -> 35.5 us  [the longest x1 8.74 us: rows_sum(): pl.pallas_call(functools.partial(rows_sum_kernel, capacity), out_shape=ja...]
    all_to_all x3 -> x2, blocking collectives: 62 us -> 33.4 us  [exchange(): return lax.all_to_all(blocks, axes, split_axis=0, concat_axis=0, tiled=True)]
    dot_general x3 -> x0, matrix products: 16.6 us -> none  [the longest x1 5.98 us: body(): lax.dot_general(masked, projection, (((1,), (1,)), ((), ())), preferred_e...]
    scatter-add x1 -> x0, other arithmetic: 13.7 us -> none  [body(): jax.ops.segment_sum(incoming.astype(jnp.float32), safe_rows, num_segments...]
    gather x2 -> x0, local copies, waits for them, and re-layouts: 9.39 us -> none  [the longest x1 6.19 us: body(): table[safe_rows]]
    scatter x2 -> x0, local copies, waits for them, and re-layouts: 8.3 us -> none  [the longest x1 4.32 us: body(): jnp.full((devices_all * capacity,), -1, jnp.int32).at[slot_index]]
    all_to_all x4 -> x2, waiting for transfers between devices: 33.4 us -> 26.6 us  [exchange(): return lax.all_to_all(blocks, axes, split_axis=0, concat_axis=0, tiled=True)]
    all_to_all x4 -> x2, starting transfers between devices: 21.5 us -> 15.7 us  [exchange(): return lax.all_to_all(blocks, axes, split_axis=0, concat_axis=0, tiled=True)]
  transfers between devices with their start and end apart: 4 -> 4, of which waited for: 3 -> 2; matrix products, arithmetic and copies ran while one was open for 16% -> 0% of each run, Pallas kernels for 0% -> 16%
where the time goes in v1:
time: 117 us
  Pallas kernels  35.5 us (30%)
  blocking collectives  33.4 us (29%)
  waiting for transfers between devices  26.6 us (23%)
  starting transfers between devices  19.1 us (16%)
  between operations  1.38 us (1%)
    all_to_all x2, blocking collectives, exchange(): return lax.all_to_all(blocks, axes, split_axis=0, concat_axis=0, tiled=True)  33.4 us
    all_to_all x2, waiting for transfers between devices, exchange(): return lax.all_to_all(blocks, axes, split_axis=0, concat_axis=0, tiled=True)  26.6 us
    all_to_all x2, starting transfers between devices, exchange(): return lax.all_to_all(blocks, axes, split_axis=0, concat_axis=0, tiled=True)  15.7 us
    pallas_call x1, Pallas kernels, rows_sum(): pl.pallas_call(functools.partial(rows_sum_kernel, capacity), out_shape=ja...  8.74 us
    pallas_call x1, Pallas kernels, front(): pl.pallas_call(functools.partial(front_kernel, shift, capacity), out_shap...  8.56 us
    pallas_call x1, Pallas kernels, hidden_rows(): pl.pallas_call(hidden_kernel, grid=(tokens // block,), out_shape=jax.Shap...  4.9 us
    pallas_call x1, Pallas kernels, picked_rows(): pl.pallas_call(functools.partial(pick_kernel, capacity), out_shape=(jax.S...  4.01 us
    pallas_call x1, Pallas kernels, first_terms(): pl.pallas_call(first_terms_kernel, in_specs=[SMEM, SMEM, VMEM, VMEM, HBM]...  3.03 us
  transfers between devices with their start and end apart: 4, of which 2 were waited for; matrix products, arithmetic and copies ran while one was open for 0% of the time, Pallas kernels for 16%

profile of v1, /device:TPU:1, one launch (start us, length us, event | category | flops | bytes accessed | tf_op | source)
XLA Modules:
  0.0 116.6 jit_solution(10618540529410032490)
XLA Ops:
  1.3 0.0 copy-start.1
  1.3 0.7 copy-done.1
  2.0 8.6 %front.1 = (s32[4,1,256]{2,1,0:T(1,128)S(1)}, bf16[2304,128]{1,0:T(8,128)(2,1)}) custom-call(s32[1]{0:T(128)S(6)} %copy.8.count_ref, s32[8,128]{1,0:T(8,128)S(1)} %bitcast.9, bf16[128,4096]{1,0:T(8,128)(2,1)} %proj_ref.1, bf16[1024,4096]{1,0:T(8,128)(2,1)} %cot_hbm.5), custom_call_target="tpu_custom_call" | custom-call | flops 1610612736 | bytes 10485760 | tf_op jit(solution)/shard_map/front/pallas_call | solution.py:131
  10.5 11.5 %all-to-all-start = ((bf16[128,9,2,128]{3,2,1,0:T(2,128)(2,1)}), bf16[128,9,2,128]{3,2,1,0:T(2,128)(2,1)S(1)}, u32[]{:S(2)}, u32[]{:S(2)}) async-start(bf16[128,9,2,128]{3,2,1,0:T(2,128)(2,1)} %bitcast.2), calls=%async_computation | async-start | bytes 1179648 | tf_op jit(solution)/shard_map/all_to_all | solution.py:50
  22.0 1.6 %held_table.1.table_ref = bf16[8192,128]{1,0:T(8,128)(2,1)S(1)} custom-call(bf16[8192,128]{1,0:T(8,128)(2,1)} %table_hbm.1), custom_call_target="tpu_custom_call" | custom-call | flops 4194304 | bytes 6291456 | tf_op jit(solution)/shard_map/held_table/pallas_call | solution.py:159
  23.6 12.9 %all-to-all-done = bf16[128,9,2,128]{3,2,1,0:T(2,128)(2,1)S(1)} async-done(((bf16[128,9,2,128]{3,2,1,0:T(2,128)(2,1)}), bf16[128,9,2,128]{3,2,1,0:T(2,128)(2,1)S(1)}, u32[]{:S(2)}, u32[]{:S(2)}) %all-to-all-start) | async-done | bytes 589856 | tf_op jit(solution)/shard_map/all_to_all | solution.py:50
  36.5 4.0 %picked_rows.1 = (bf16[2048,128]{1,0:T(8,128)(2,1)}, s32[16,128]{1,0:T(8,128)S(1)}) custom-call(bf16[2304,128]{1,0:T(8,128)(2,1)S(1)} %bitcast.6, bf16[8192,128]{1,0:T(8,128)(2,1)S(1)} %held_table.1.table_ref), custom_call_target="tpu_custom_call" | custom-call | flops 67108864 | bytes 3145728 | tf_op jit(solution)/shard_map/picked_rows/pallas_call | solution.py:203
  40.5 4.3 %all-to-all-start.1 = ((bf16[128,16,128]{2,1,0:T(8,128)(2,1)}), bf16[128,16,128]{2,1,0:T(8,128)(2,1)S(1)}, u32[]{:S(2)}, u32[]{:S(2)}) async-start(bf16[128,16,128]{2,1,0:T(8,128)(2,1)} %bitcast.4), calls=%async_computation.1 | async-start | bytes 1048576 | tf_op jit(solution)/shard_map/all_to_all | solution.py:50
  44.8 13.8 %all-to-all-done.1 = bf16[128,16,128]{2,1,0:T(8,128)(2,1)S(1)} async-done(((bf16[128,16,128]{2,1,0:T(8,128)(2,1)}), bf16[128,16,128]{2,1,0:T(8,128)(2,1)S(1)}, u32[]{:S(2)}, u32[]{:S(2)}) %all-to-all-start.1) | async-done | bytes 524320 | tf_op jit(solution)/shard_map/all_to_all | solution.py:50
  58.5 3.0 %first_terms.1 = (bf16[128,1024]{1,0:T(8,128)(2,1)S(1)}, f32[128,2048]{1,0:T(8,128)S(1)}) custom-call(s32[1]{0:T(128)S(6)} %sub.3.half_ref, s32[1]{0:T(128)S(6)} %copy.8.count_ref, s32[4,1,256]{2,1,0:T(1,128)S(1)} %get-tuple-element.9.slot_ref, bf16[2048,128]{1,0:T(8,128)(2,1)S(1)} %bitcast.8, bf16[1024,4096]{1,0:T(8,128)(2,1)} %cot_hbm.5), custom_call_target="tpu_custom_call" | custom-call | flops 805306368 | bytes 6291456 | tf_op jit(solution)/shard_map/first_terms/pallas_call | solution.py:322
  61.6 0.5 collective-permute-start
  62.1 2.9 %half_terms.1.mine_ref = f32[128,2048]{1,0:T(8,128)S(1)} custom-call(s32[1]{0:T(128)} %bitcast.half_ref.core_ref, bf16[128,1024]{1,0:T(8,128)(2,1)S(1)} %get-tuple-element.12.emb_ref, bf16[1024,4096]{1,0:T(8,128)(2,1)} %cot_hbm.5), custom_call_target="tpu_custom_call" | custom-call | flops 536870912 | bytes 5242880 | tf_op jit(solution)/shard_map/half_terms/pallas_call | solution.py:343
  65.0 0.0 collective-permute-done.other_ref
  65.0 0.1 chip_parts.1
  65.1 0.0 copy-start
  65.1 17.5 %all_to_all.20.parts_ref = bf16[64,32,128]{2,1,0:T(8,128)(2,1)S(1)} all-to-all(bf16[64,32,128]{2,1,0:T(8,128)(2,1)S(1)} %chip_parts.1), channel_id=1, replica_groups=mesh['vocab_0'=4,'vocab_1'=4,'vocab_2'=2,'dp'=4] {'vocab_0','vocab_1','dp'}, dimensions={0} | all-to-all | bytes 1048576 | tf_op jit(solution)/shard_map/all_to_all | solution.py:50
  82.7 0.1 chips_total.1
  82.8 15.9 %all_to_all.21.mine_ref = bf16[64,32,128]{2,1,0:T(8,128)(2,1)S(1)} all-to-all(bf16[64,32,128]{2,1,0:T(8,128)(2,1)S(1)} %chips_total.1), channel_id=1, replica_groups=mesh['vocab_0'=4,'vocab_1'=4,'vocab_2'=2,'dp'=4] {'vocab_0','vocab_1','dp'}, dimensions={0} | all-to-all | bytes 1048576 | tf_op jit(solution)/shard_map/all_to_all | solution.py:50
  98.7 2.8 %collective-permute-start.1 = (bf16[64,32,128]{2,1,0:T(8,128)(2,1)S(1)}, bf16[64,32,128]{2,1,0:T(8,128)(2,1)S(1)}, u32[]{:S(2)}, u32[]{:S(2)}) collective-permute-start(bf16[64,32,128]{2,1,0:T(8,128)(2,1)S(1)} %all_to_all.21.mine_ref), channel_id=1, source_target_pairs={{0,4},{4,0},{1,5},{5,1},{2,6},{6,2},{3,7},{7,3},{8,12},{12,8},{9,1... | collective-permute-start | bytes 1572872 | tf_op jit(solution)/shard_map/ppermute | solution.py:479
  101.5 8.7 %rows_sum.1 = f32[8192,128]{1,0:T(8,128)} custom-call(s32[16,128]{1,0:T(8,128)S(1)} %get-tuple-element.14.index_ref, bf16[2304,128]{1,0:T(8,128)(2,1)S(1)} %bitcast.7), custom_call_target="tpu_custom_call" | custom-call | flops 268435456 | bytes 6291456 | tf_op jit(solution)/shard_map/rows_sum/pallas_call | solution.py:254
  110.2 0.0 copy-done
  110.2 4.9 %hidden_rows.1 = bf16[1024,4096]{1,0:T(8,128)(2,1)} custom-call(bf16[128,1024]{1,0:T(8,128)(2,1)S(1)} %get-tuple-element.12.emb_ref, bf16[128,4096]{1,0:T(8,128)(2,1)S(1)} %copy-done), custom_call_target="tpu_custom_call" | custom-call | flops 1073741824 | bytes 9437184 | tf_op jit(solution)/shard_map/hidden_rows/pallas_call | solution.py:443
  115.1 0.0 collective-permute-done.1.other_ref
  115.1 1.5 %result.1 = f32[128,4096]{1,0:T(8,128)} custom-call(s32[1]{0:T(128)} %bitcast.half_ref.core_ref, bf16[64,32,128]{2,1,0:T(8,128)(2,1)S(1)} %all_to_all.21.mine_ref, bf16[64,32,128]{2,1,0:T(8,128)(2,1)S(1)} %collective-permute-done.1.other_ref), custom_call_target="tpu_custom_call" | custom-call | flops 16777216 | bytes 3145728 | tf_op jit(solution)/shard_map/result/pallas_call | solution.py:424
Async XLA Ops:
  1.3 0.7 copy-start.1
  10.5 26.0 %all-to-all-start = ((bf16[128,9,2,128]{3,2,1,0:T(2,128)(2,1)}), bf16[128,9,2,128]{3,2,1,0:T(2,128)(2,1)S(1)}, u32[]{:S(2)}, u32[]{:S(2)}) async-start(bf16[128,9,2,128]{3,2,1,0:T(2,128)(2,1)} %bitcast.2), calls=%async_computation | async-start | bytes 1179648 | tf_op jit(solution)/shard_map/all_to_all | solution.py:50
  40.5 18.0 %all-to-all-start.1 = ((bf16[128,16,128]{2,1,0:T(8,128)(2,1)}), bf16[128,16,128]{2,1,0:T(8,128)(2,1)S(1)}, u32[]{:S(2)}, u32[]{:S(2)}) async-start(bf16[128,16,128]{2,1,0:T(8,128)(2,1)} %bitcast.4), calls=%async_computation.1 | async-start | bytes 1048576 | tf_op jit(solution)/shard_map/all_to_all | solution.py:50
  61.6 3.4 %collective-permute-start = (f32[128,2048]{1,0:T(8,128)S(1)}, f32[128,2048]{1,0:T(8,128)S(1)}, u32[]{:S(2)}, u32[]{:S(2)}) collective-permute-start(f32[128,2048]{1,0:T(8,128)S(1)} %get-tuple-element.13), channel_id=1, source_target_pairs={{0,4},{4,0},{1,5},{5,1},{2,6},{6,2},{3,7},{7,3},{8,12},{12,8},{9,1... | collective-permute-start | bytes 3145736 | tf_op jit(solution)/shard_map/ppermute | solution.py:472
  65.1 45.1 %copy-start = (bf16[128,4096]{1,0:T(8,128)(2,1)S(1)}, bf16[128,4096]{1,0:T(8,128)(2,1)}, u32[]{:S(2)}) copy-start(bf16[128,4096]{1,0:T(8,128)(2,1)} %proj_ref.1) | copy-start | bytes 3145732
  98.7 16.5 %collective-permute-start.1 = (bf16[64,32,128]{2,1,0:T(8,128)(2,1)S(1)}, bf16[64,32,128]{2,1,0:T(8,128)(2,1)S(1)}, u32[]{:S(2)}, u32[]{:S(2)}) collective-permute-start(bf16[64,32,128]{2,1,0:T(8,128)(2,1)S(1)} %all_to_all.21.mine_ref), channel_id=1, source_target_pairs={{0,4},{4,0},{1,5},{5,1},{2,6},{6,2},{3,7},{7,3},{8,12},{12,8},{9,1... | collective-permute-start | bytes 1572872 | tf_op jit(solution)/shard_map/ppermute | solution.py:479

commit v2 on v1

v2 whole, which is shorter than its diff:
```python
import functools
import math

import jax
import jax.numpy as jnp
from jax import lax
from jax.experimental import pallas as pl
from jax.experimental.pallas import tpu as pltpu
from jax.sharding import Mesh
from jax.sharding import PartitionSpec as P


ALL = ("vocab_0", "vocab_1", "vocab_2", "dp")
CHIPS = ("vocab_0", "vocab_1", "dp")
CORE = "vocab_2"
SWAP = ((0, 1), (1, 0))
LANES = 128
BF16 = jnp.bfloat16
F32 = jnp.float32
VMEM = pl.BlockSpec(memory_space=pltpu.VMEM)
SMEM = pl.BlockSpec(memory_space=pltpu.SMEM)
HBM = pl.BlockSpec(memory_space=pltpu.HBM)


def in_hbm(x):
    return pltpu.with_memory_space_constraint(x, pltpu.HBM)


def in_vmem(x):
    return pltpu.with_memory_space_constraint(x, pltpu.VMEM)


def params(mib):
    return pltpu.CompilerParams(vmem_limit_bytes=mib << 20)


def cost(flops, nbytes):
    return pl.CostEstimate(flops=flops, bytes_accessed=nbytes, transcendentals=0)


def dot(a, b, dims=((1,), (0,))):
    return lax.dot_general(a, b, (dims, ((), ())), preferred_element_type=F32)


def one_hot(hit):
    return jnp.where(hit, 1.0, 0.0).astype(BF16)


def exchange(blocks, axes):
    return lax.all_to_all(blocks, axes, split_axis=0, concat_axis=0, tiled=True)


def prepare_kernel(shift, capacity, core_ref, count_ref, ids_ref, slot_ref, request_ref):
    del core_ref, count_ref
    n = request_ref.shape[0]
    chunks, lanes = ids_ref.shape
    holder = lax.broadcasted_iota(jnp.int32, (n, lanes), 0)
    before = one_hot(
        lax.broadcasted_iota(jnp.int32, (lanes, lanes), 0)
        < lax.broadcasted_iota(jnp.int32, (lanes, lanes), 1)
    )
    place = lax.broadcasted_iota(jnp.int32, (capacity, lanes), 0)
    seen = jnp.zeros((n, 1), F32)
    high = jnp.zeros((n, capacity), F32)
    low = jnp.zeros((n, capacity), F32)
    ids = ids_ref[...]
    owner = lax.shift_right_logical(ids, shift)
    row = ids & ((1 << shift) - 1)
    for k in range(chunks):
        own = owner[k : k + 1, :]
        hit = holder == own
        hits = one_hot(hit)
        earlier = dot(hits, before) + seen
        rank = jnp.sum(jnp.where(hit, earlier, 0.0), axis=0, keepdims=True).astype(jnp.int32)
        seen = seen + jnp.sum(jnp.where(hit, 1.0, 0.0), axis=1, keepdims=True)
        per = slot_ref.shape[2] // lanes
        slot_ref[k // per, :, (k % per) * lanes : (k % per + 1) * lanes] = own * capacity + rank
        mine = place == rank
        line = row[k : k + 1, :]
        upper = lax.shift_right_logical(line, 7).astype(F32)
        lower = (line & 127).astype(F32)
        high = high + dot(hits, jnp.where(mine, upper, 0.0).astype(BF16), ((1,), (1,)))
        low = low + dot(hits, jnp.where(mine, lower, 0.0).astype(BF16), ((1,), (1,)))
    request_ref[...] = (high * 128.0 + low).astype(jnp.int32)


def prepare(core, counts, token_ids, held_rows, n, capacity, block):
    tokens = token_ids.shape[0]
    shift = held_rows.bit_length() - 1
    assert held_rows == 1 << shift and shift <= 15
    return pl.pallas_call(
        functools.partial(prepare_kernel, shift, capacity),
        out_shape=(
            jax.ShapeDtypeStruct((tokens // block, 1, block), jnp.int32),
            jax.ShapeDtypeStruct((n, capacity), jnp.int32),
        ),
        in_specs=[SMEM, SMEM, VMEM],
        out_specs=(VMEM, VMEM),
        compiler_params=params(8),
        cost_estimate=cost(1 << 26, 1 << 16),
        name="prepare",
    )(core, counts, token_ids.reshape(tokens // LANES, LANES))


def grads_kernel(
    count_ref, slot_ref, proj_hbm, cot_hbm, table_hbm, out_ref, table, cot, proj, across, grads, sems
):
    steps, _, block = slot_ref.shape
    proj_copy = pltpu.make_async_copy(proj_hbm, proj, sems.at[steps])
    proj_copy.start()
    copies = []
    for i in range(steps):
        rows = pl.ds(i * block, block)
        copies.append(pltpu.make_async_copy(cot_hbm.at[rows, :], cot.at[rows, :], sems.at[i]))
        copies[-1].start()
    table_copy = pltpu.make_async_copy(table_hbm, table, sems.at[steps + 1])
    table_copy.start()
    proj_copy.wait()
    across[...] = proj[...].T
    for i in range(steps):
        copies[i].wait()
        rows = slice(i * block, (i + 1) * block)
        grad = dot(cot[rows, :], across[...])
        token = lax.broadcasted_iota(jnp.int32, grad.shape, 0) + i * block
        grads[rows, :] = jnp.where(token < count_ref[0], grad, 0.0).astype(BF16)
    step = 256
    line = lax.broadcasted_iota(jnp.int32, (step, block), 0)
    for c in range(out_ref.shape[0] // step):
        total = jnp.zeros((step, out_ref.shape[1]), F32)
        for k in range(steps):
            hit = line == slot_ref[k] - c * step
            total += dot(one_hot(hit), grads[k * block : (k + 1) * block, :])
        out_ref[c * step : (c + 1) * step, :] = total.astype(BF16)
    table_copy.wait()


def placed_grads(counts, slots, projection, cotangent, table, n_slots):
    tokens, hidden = cotangent.shape
    width = projection.shape[0]
    return pl.pallas_call(
        grads_kernel,
        out_shape=(
            jax.ShapeDtypeStruct((n_slots, width), BF16),
            pltpu.VMEM(table.shape, table.dtype),
        ),
        in_specs=[SMEM, VMEM, HBM, HBM, HBM],
        out_specs=(VMEM, VMEM),
        scratch_shapes=[
            pltpu.VMEM((tokens, hidden), BF16),
            pltpu.VMEM((width, hidden), BF16),
            pltpu.VMEM((hidden, width), BF16),
            pltpu.VMEM((tokens, width), BF16),
            pltpu.SemaphoreType.DMA((slots.shape[0] + 2,)),
        ],
        compiler_params=params(24),
        cost_estimate=cost(3 << 29, 10 << 20),
        name="placed_grads",
    )(counts, slots, in_hbm(projection), in_hbm(cotangent), in_hbm(table))


def pick_kernel(index_ref, grads_ref, held_ref, out_ref, index, table, stage, sem):
    copy = pltpu.make_async_copy(index_ref, index, sem)
    copy.start()
    n, _, capacity = index_ref.shape
    for p in range(n):
        out_ref[p, capacity:, :] = grads_ref[p * capacity : (p + 1) * capacity, :]
    step = 256

    @pl.loop(0, table.shape[0] // step)
    def _(c):
        rows = pl.ds(pl.multiple_of(c * step, step), step)
        table[rows, :] = held_ref[rows, :].astype(F32)

    copy.wait()
    unroll = 4

    @pl.loop(0, n // unroll)
    def _(q):
        for k in range(unroll):
            p = q * unroll + k
            for r in range(capacity):
                stage[pl.ds(p * capacity + r, 1), :] = table[pl.ds(index[p, 0, r], 1), :]

    for p in range(n):
        out_ref[p, :capacity, :] = stage[p * capacity : (p + 1) * capacity, :].astype(BF16)


def picked_rows(received, outgoing, held):
    n, _, capacity = received.shape
    slots = n * capacity
    rows, width = held.shape
    return pl.pallas_call(
        pick_kernel,
        out_shape=jax.ShapeDtypeStruct((n, 2 * capacity, width), BF16),
        in_specs=[VMEM, VMEM, VMEM],
        out_specs=VMEM,
        scratch_shapes=[
            pltpu.SMEM(received.shape, jnp.int32),
            pltpu.VMEM((rows, width), F32),
            pltpu.VMEM((slots, width), F32),
            pltpu.SemaphoreType.DMA(()),
        ],
        compiler_params=params(14),
        cost_estimate=cost(1 << 26, 3 << 20),
        name="picked_rows",
    )(received, outgoing, in_vmem(held))


def rows_sum_kernel(index_ref, grads_ref, out_hbm, index, wide, first, *rest):
    *others, index_sem, sems = rest
    copy = pltpu.make_async_copy(index_ref, index, index_sem)
    copy.start()
    sums = (first, *others)
    held, width = first.shape
    step = 256

    @pl.loop(0, held // step)
    def _(c):
        rows = pl.ds(pl.multiple_of(c * step, step), step)
        for total in sums:
            total[rows, :] = jnp.zeros((step, width), F32)

    n, _, capacity = index_ref.shape
    for p in range(n):
        wide[p * capacity : (p + 1) * capacity, :] = grads_ref[p, capacity:, :].astype(F32)
    copy.wait()
    share = n // len(sums)

    @pl.loop(0, share)
    def _(q):
        for r in range(capacity):
            for s, total in enumerate(sums):
                p = q + s * share
                row = pl.ds(index[p, 0, r], 1)
                total[row, :] += wide[pl.ds(p * capacity + r, 1), :]

    steps = sems.shape[0]
    block = held // steps
    copies = []
    for i in range(steps):

        @pl.loop(i * block // step, (i + 1) * block // step)
        def _(c):
            rows = pl.ds(pl.multiple_of(c * step, step), step)
            first[rows, :] = (first[rows, :] + others[0][rows, :]) + (
                others[1][rows, :] + others[2][rows, :]
            )

        rows = pl.ds(i * block, block)
        copies.append(pltpu.make_async_copy(first.at[rows, :], out_hbm.at[rows, :], sems.at[i]))
        copies[-1].start()
    for copy in copies:
        copy.wait()


def rows_sum(received, arrived, held_rows):
    n, _, capacity = received.shape
    width = arrived.shape[2]
    total = pltpu.VMEM((held_rows, width), F32)
    return pl.pallas_call(
        rows_sum_kernel,
        out_shape=jax.ShapeDtypeStruct((held_rows, width), F32),
        in_specs=[VMEM, VMEM],
        out_specs=HBM,
        scratch_shapes=[
            pltpu.SMEM(received.shape, jnp.int32),
            pltpu.VMEM((n * capacity, width), F32),
            total,
            total,
            total,
            total,
            pltpu.SemaphoreType.DMA(()),
            pltpu.SemaphoreType.DMA((4,)),
        ],
        compiler_params=params(24),
        cost_estimate=cost(1 << 28, 6 << 20),
        name="rows_sum",
    )(received, arrived)


def cot_copies(half, cot_hbm, cot, sems):
    tokens, wide = cot.shape
    steps = sems.shape[0]
    block = tokens // steps
    columns = pl.ds(pl.multiple_of(half * wide, wide), wide)
    copies = []
    for i in range(steps):
        rows = pl.ds(i * block, block)
        copies.append(
            pltpu.make_async_copy(cot_hbm.at[rows, columns], cot.at[rows, :], sems.at[i])
        )
        copies[-1].start()
    return copies


def add_terms(emb, cot, i, out_ref):
    tokens = emb.shape[1]
    block = 512
    for c in range(out_ref.shape[1] // block):
        columns = slice(c * block, (c + 1) * block)
        part = dot(emb, cot[i * tokens : (i + 1) * tokens, columns])
        if i == 0:
            out_ref[:, columns] = part
        else:
            out_ref[:, columns] += part


def terms_kernel(core_ref, emb_ref, cot_hbm, out_ref, cot, sems):
    copies = cot_copies(core_ref[0], cot_hbm, cot, sems)
    block = emb_ref.shape[1] // len(copies)
    for i, copy in enumerate(copies):
        copy.wait()
        add_terms(emb_ref[:, i * block : (i + 1) * block], cot, i, out_ref)


def first_terms_kernel(
    core_ref, count_ref, slot_ref, rows_ref, cot_hbm, emb_ref, out_ref, cot, sems
):
    copies = cot_copies(1 - core_ref[0], cot_hbm, cot, sems)
    chunks, _, block = slot_ref.shape
    n, double, width = rows_ref.shape
    n_slots = n * double // 2
    across = rows_ref[:, : double // 2, :].reshape(n_slots, width).T
    step = 256
    line = lax.broadcasted_iota(jnp.int32, (step, block), 0)
    for k in range(chunks):
        slot = slot_ref[k]
        total = jnp.zeros((width, block), F32)
        for c in range(n_slots // step):
            total += dot(across[:, c * step : (c + 1) * step], one_hot(line + c * step == slot))
        token = lax.broadcasted_iota(jnp.int32, total.shape, 1) + k * block
        emb = jnp.where(token < count_ref[0], total, 0.0).astype(BF16)
        emb_ref[:, k * block : (k + 1) * block] = emb
        copies[k].wait()
        add_terms(emb, cot, k, out_ref)


def first_terms(core, counts, slots, returned, cotangent):
    tokens, hidden = cotangent.shape
    width = returned.shape[2]
    return pl.pallas_call(
        first_terms_kernel,
        in_specs=[SMEM, SMEM, VMEM, VMEM, HBM],
        out_specs=(VMEM, VMEM),
        scratch_shapes=[
            pltpu.VMEM((tokens, hidden // 2), BF16),
            pltpu.SemaphoreType.DMA((4,)),
        ],
        out_shape=(
            jax.ShapeDtypeStruct((width, tokens), BF16),
            jax.ShapeDtypeStruct((width, hidden // 2), F32),
        ),
        compiler_params=params(16),
        cost_estimate=cost(3 << 28, 6 << 20),
        name="first_terms",
    )(core, counts, slots, returned, in_hbm(cotangent))


def half_terms(core, embedded, cotangent):
    tokens, hidden = cotangent.shape
    width = embedded.shape[0]
    return pl.pallas_call(
        terms_kernel,
        in_specs=[SMEM, VMEM, HBM],
        out_specs=VMEM,
        scratch_shapes=[
            pltpu.VMEM((tokens, hidden // 2), BF16),
            pltpu.SemaphoreType.DMA((4,)),
        ],
        out_shape=jax.ShapeDtypeStruct((width, hidden // 2), F32),
        compiler_params=params(16),
        cost_estimate=cost(1 << 29, 5 << 20),
        name="half_terms",
    )(core, embedded, in_hbm(cotangent))


def parts_kernel(tiles, mine_ref, other_ref, out_ref):
    groups = mine_ref.shape[1] // (tiles * LANES)
    for g in range(mine_ref.shape[0] // 8):
        rows = slice(8 * g, 8 * g + 8)
        for j in range(groups):
            columns = slice(j * tiles * LANES, (j + 1) * tiles * LANES)
            total = mine_ref[rows, columns] + other_ref[rows, columns]
            block = [total[:, t * LANES : (t + 1) * LANES] for t in range(tiles)]
            out_ref[g * groups + j] = jnp.concatenate(block, axis=0).astype(BF16)


def chip_parts(mine, other, chips):
    rows, columns = mine.shape
    tiles = rows * columns // (8 * LANES * chips)
    return pl.pallas_call(
        functools.partial(parts_kernel, tiles),
        out_shape=jax.ShapeDtypeStruct((chips, 8 * tiles, LANES), BF16),
        in_specs=[VMEM, VMEM],
        out_specs=VMEM,
        compiler_params=params(8),
        cost_estimate=cost(1 << 24, 3 << 20),
        name="chip_parts",
    )(mine, other)


def total_kernel(parts_ref, out_ref):
    total = parts_ref[0].astype(F32)
    for p in range(1, parts_ref.shape[0]):
        total += parts_ref[p].astype(F32)
    total = total.astype(BF16)
    for p in range(out_ref.shape[0]):
        out_ref[p] = total


def chips_total(parts):
    return pl.pallas_call(
        total_kernel,
        out_shape=jax.ShapeDtypeStruct(parts.shape, BF16),
        in_specs=[VMEM],
        out_specs=VMEM,
        compiler_params=params(8),
        cost_estimate=cost(1 << 24, 1 << 20),
        name="chips_total",
    )(parts)


def result_kernel(tiles, scaling, own, core_ref, source_ref, *rest):
    out_hbm, half, sems = rest[-3:]
    core = core_ref[0] if own else 1 - core_ref[0]
    rows, wide = half.shape
    groups = wide // (tiles * LANES)
    columns = pl.ds(pl.multiple_of(core * wide, wide), wide)
    steps = sems.shape[0]
    block = rows // steps
    copies = []
    for i in range(steps):
        for g in range(i * block // 8, (i + 1) * block // 8):
            for j in range(groups):
                part = source_ref[g * groups + j].astype(F32) * scaling
                for t in range(tiles):
                    left = (j * tiles + t) * LANES
                    half[8 * g : 8 * g + 8, left : left + LANES] = part[8 * t : 8 * t + 8, :]
        lines = pl.ds(i * block, block)
        target = out_hbm.at[lines, columns]
        copies.append(pltpu.make_async_copy(half.at[lines, :], target, sems.at[i]))
        copies[-1].start()
    for copy in copies:
        copy.wait()


def result_half(own, core, source, before, width, hidden, scaling):
    tiles = source.shape[1] // 8
    steps = 4
    return pl.pallas_call(
        functools.partial(result_kernel, tiles, scaling, own),
        out_shape=jax.ShapeDtypeStruct((width, hidden), F32),
        in_specs=[SMEM, VMEM] + [HBM] * len(before),
        out_specs=HBM,
        input_output_aliases={2: 0} if before else {},
        scratch_shapes=[
            pltpu.VMEM((width, hidden // 2), F32),
            pltpu.SemaphoreType.DMA((steps,)),
        ],
        compiler_params=params(8),
        cost_estimate=cost(1 << 24, 3 << 20),
        name="own_result" if own else "result",
    )(core, source, *before)


def hidden_kernel(emb_ref, proj_ref, out_ref):
    out_ref[...] = dot(emb_ref[...].T, proj_ref[...]).astype(BF16)


def hidden_rows(embedded, projection):
    width, tokens = embedded.shape
    hidden = projection.shape[1]
    block = 256
    return pl.pallas_call(
        hidden_kernel,
        grid=(tokens // block,),
        out_shape=jax.ShapeDtypeStruct((tokens, hidden), BF16),
        in_specs=[
            pl.BlockSpec((width, block), lambda i: (0, i)),
            pl.BlockSpec((width, hidden), lambda i: (0, 0)),
        ],
        out_specs=pl.BlockSpec((block, hidden), lambda i: (i, 0)),
        compiler_params=params(16),
        cost_estimate=cost(1 << 30, 9 << 20),
        name="hidden_rows",
    )(embedded, projection)


def body(token_ids, counts, table, projection, cotangent):
    tokens = token_ids.shape[0]
    held_rows, width = table.shape
    hidden_width = projection.shape[1]
    n = lax.axis_size(ALL)
    chips = lax.axis_size(CHIPS)
    capacity = 2 * tokens // n
    core = lax.axis_index(CORE).astype(jnp.int32).reshape(1)
    slots, requests = prepare(core, counts, token_ids, held_rows, n, capacity, 256)
    received = exchange(requests.reshape(n, 1, capacity), ALL)
    outgoing, held = placed_grads(
        counts, slots, projection, cotangent, table, n * capacity
    )
    picked = picked_rows(received, outgoing, held)
    returned = exchange(picked, ALL)
    embedded, theirs = first_terms(core, counts, slots, returned, cotangent)
    other = lax.ppermute(theirs, CORE, SWAP)
    mine = half_terms(core, embedded, cotangent)
    parts = chip_parts(mine, other, chips)
    arrived = exchange(parts, CHIPS)
    hidden = hidden_rows(embedded, projection)
    total = chips_total(arrived)
    whole = exchange(total, CHIPS)
    across = lax.ppermute(whole, CORE, SWAP)
    scaling = 1.0 / math.sqrt(tokens * n)
    partial = result_half(True, core, whole, (), width, hidden_width, scaling)
    grad_projection = result_half(False, core, across, (partial,), width, hidden_width, scaling)
    grad_table = rows_sum(received, returned, held_rows)
    return (hidden, grad_projection, grad_table)


def solution(mesh):
    finer = Mesh(
        mesh.devices.reshape(4, 4, 2, mesh.shape["dp"]), ("vocab_0", "vocab_1", "vocab_2", "dp")
    )
    in_specs = (P(ALL), P(ALL), P(ALL, None), P(), P(ALL, None))
    out_specs = (P(ALL, None), P(), P(ALL, None))
    return jax.shard_map(body, mesh=finer, in_specs=in_specs, out_specs=out_specs, check_vma=False)
```

time: 117 us -> 111 us (0.949)
  blocking collectives: 33.4 us -> 58.3 us
  waiting for transfers between devices: 26.6 us -> 3.65 us
  starting transfers between devices: 19.1 us -> 14.8 us
  Pallas kernels: 35.5 us -> 31.8 us
    all_to_all x2 -> x3, blocking collectives: 33.4 us -> 58.3 us  [exchange(): return lax.all_to_all(blocks, axes, split_axis=0, concat_axis=0, tiled=True)]
    all_to_all x2 -> x1, waiting for transfers between devices: 26.6 us -> 3.65 us  [exchange(): return lax.all_to_all(blocks, axes, split_axis=0, concat_axis=0, tiled=True)]
    all_to_all x2 -> x1, starting transfers between devices: 15.7 us -> 11.5 us  [exchange(): return lax.all_to_all(blocks, axes, split_axis=0, concat_axis=0, tiled=True)]
    pallas_call x5 -> x6, Pallas kernels: 24.4 us -> 21.2 us  [the longest x1 7.8 us: rows_sum(): pl.pallas_call(rows_sum_kernel, out_shape=jax.ShapeDtypeStruct((held_rows...]
  transfers between devices with their start and end apart: 4 -> 3, of which waited for: 2 -> 1; matrix products, arithmetic and copies ran while one was open for 0% -> 0% of each run, Pallas kernels for 16% -> 20%
where the time goes in v2:
time: 111 us
  blocking collectives  58.3 us (53%)
  Pallas kernels  31.8 us (29%)
  starting transfers between devices  14.8 us (13%)
  waiting for transfers between devices  3.65 us (3%)
  between operations  1.38 us (1%)
    all_to_all x3, blocking collectives, exchange(): return lax.all_to_all(blocks, axes, split_axis=0, concat_axis=0, tiled=True)  58.3 us
    all_to_all x1, starting transfers between devices, exchange(): return lax.all_to_all(blocks, axes, split_axis=0, concat_axis=0, tiled=True)  11.5 us
    pallas_call x1, Pallas kernels, rows_sum(): pl.pallas_call(rows_sum_kernel, out_shape=jax.ShapeDtypeStruct((held_rows...  7.8 us
    pallas_call x1, Pallas kernels, placed_grads(): pl.pallas_call(grads_kernel, out_shape=(jax.ShapeDtypeStruct((n_slots, wi...  5.94 us
    pallas_call x1, Pallas kernels, hidden_rows(): pl.pallas_call(hidden_kernel, grid=(tokens // block,), out_shape=jax.Shap...  4.89 us
    all_to_all x1, waiting for transfers between devices, exchange(): return lax.all_to_all(blocks, axes, split_axis=0, concat_axis=0, tiled=True)  3.65 us
    pallas_call x1, Pallas kernels, picked_rows(): pl.pallas_call(pick_kernel, out_shape=jax.ShapeDtypeStruct((n, 2 * capaci...  3.42 us
    pallas_call x1, Pallas kernels, first_terms(): pl.pallas_call(first_terms_kernel, in_specs=[SMEM, SMEM, VMEM, VMEM, HBM]...  2.97 us
  transfers between devices with their start and end apart: 3, of which 1 were waited for; matrix products, arithmetic and copies ran while one was open for 0% of the time, Pallas kernels for 20%

profile of v2, /device:TPU:1, one launch (start us, length us, event | category | flops | bytes accessed | tf_op | source)
XLA Modules:
  0.0 110.6 jit_solution(6385050817241461492)
XLA Ops:
  1.3 0.0 copy-start.1
  1.3 0.7 copy-done.1
  2.0 2.0 %prepare.1 = (s32[4,1,256]{2,1,0:T(1,128)S(1)}, s32[128,16]{1,0:T(8,128)}) custom-call(s32[1]{0:T(128)} %bitcast.core_ref, s32[1]{0:T(128)S(6)} %copy.10.count_ref, s32[8,128]{1,0:T(8,128)S(1)} %bitcast.3), custom_call_target="tpu_custom_call" | custom-call | flops 67108864 | bytes 65536 | tf_op jit(solution)/shard_map/prepare/pallas_call | solution.py:91
  4.0 11.5 %all-to-all-start = ((s32[128,1,16]{2,1,0:T(1,128)}), s32[128,1,16]{2,1,0:T(1,128)S(1)}, u32[]{:S(2)}, u32[]{:S(2)}) async-start(s32[128,1,16]{2,1,0:T(1,128)} %bitcast.2), calls=%async_computation | async-start | bytes 131072 | tf_op jit(solution)/shard_map/all_to_all | solution.py:50
  15.5 5.9 %placed_grads.1 = (bf16[2048,128]{1,0:T(8,128)(2,1)S(1)}, bf16[8192,128]{1,0:T(8,128)(2,1)S(1)}) custom-call(s32[1]{0:T(128)S(6)} %copy.10.count_ref, s32[4,1,256]{2,1,0:T(1,128)S(1)} %get-tuple-element.9.slot_ref, bf16[128,4096]{1,0:T(8,128)(2,1)} %proj_ref.1, bf16[1024,4096]{1,0:T(8,128)(2,1)} %cot_hbm.5, bf16[8192,128]{1,0:T(8,128)(2,1)} %table_hbm.1), custom_call_target="tpu_custom_call" | custom-call | flops 1610612736 | bytes 10485760 | tf_op jit(solution)/shard_map/placed_grads/pallas_call | solution.py:140
  21.4 3.6 %all-to-all-done.index_ref = s32[128,1,16]{2,1,0:T(1,128)S(1)} async-done(((s32[128,1,16]{2,1,0:T(1,128)}), s32[128,1,16]{2,1,0:T(1,128)S(1)}, u32[]{:S(2)}, u32[]{:S(2)}) %all-to-all-start) | async-done | bytes 8224 | tf_op jit(solution)/shard_map/all_to_all | solution.py:50
  25.1 3.4 %picked_rows.1 = bf16[128,32,128]{2,1,0:T(8,128)(2,1)S(1)} custom-call(s32[128,1,16]{2,1,0:T(1,128)S(1)} %all-to-all-done.index_ref, bf16[2048,128]{1,0:T(8,128)(2,1)S(1)} %get-tuple-element.11.grads_ref, bf16[8192,128]{1,0:T(8,128)(2,1)S(1)} %get-tuple-element.12.held_ref), custom_call_target="tpu_custom_call" | custom-call | flops 67108864 | bytes 3145728 | tf_op jit(solution)/shard_map/picked_rows/pallas_call | solution.py:192
  28.5 25.2 %all_to_all.20.rows_ref.grads_ref = bf16[128,32,128]{2,1,0:T(8,128)(2,1)S(1)} all-to-all(bf16[128,32,128]{2,1,0:T(8,128)(2,1)S(1)} %picked_rows.1), channel_id=1, replica_groups=mesh['vocab_0'=4,'vocab_1'=4,'vocab_2'=2,'dp'=4] {'vocab_0','vocab_1','v..., dimensions={0} | all-to-all | bytes 2097152 | tf_op jit(solution)/shard_map/all_to_all | solution.py:50
  53.7 3.0 %first_terms.1 = (bf16[128,1024]{1,0:T(8,128)(2,1)S(1)}, f32[128,2048]{1,0:T(8,128)S(1)}) custom-call(s32[1]{0:T(128)} %bitcast.core_ref, s32[1]{0:T(128)S(6)} %copy.10.count_ref, s32[4,1,256]{2,1,0:T(1,128)S(1)} %get-tuple-element.9.slot_ref, bf16[128,32,128]{2,1,0:T(8,128)(2,1)S(1)} %all_to_all.20.rows_ref.grads_ref, bf16[1024,4096]{1,0:T(8,128)(2,1)} %cot_hbm.5), custom_call_target="tpu_custom_call" | custom-call | flops 805306368 | bytes 6291456 | tf_op jit(solution)/shard_map/first_terms/pallas_call | solution.py:341
  56.7 0.5 collective-permute-start
  57.2 2.5 %half_terms.1.mine_ref = f32[128,2048]{1,0:T(8,128)S(1)} custom-call(s32[1]{0:T(128)} %bitcast.core_ref, bf16[128,1024]{1,0:T(8,128)(2,1)S(1)} %get-tuple-element.13.emb_ref, bf16[1024,4096]{1,0:T(8,128)(2,1)} %cot_hbm.5), custom_call_target="tpu_custom_call" | custom-call | flops 536870912 | bytes 5242880 | tf_op jit(solution)/shard_map/half_terms/pallas_call | solution.py:362
  59.7 0.0 collective-permute-done.other_ref
  59.7 0.1 chip_parts.1
  59.8 17.2 %all_to_all.21.parts_ref = bf16[64,32,128]{2,1,0:T(8,128)(2,1)S(1)} all-to-all(bf16[64,32,128]{2,1,0:T(8,128)(2,1)S(1)} %chip_parts.1), channel_id=1, replica_groups=mesh['vocab_0'=4,'vocab_1'=4,'vocab_2'=2,'dp'=4] {'vocab_0','vocab_1','dp'}, dimensions={0} | all-to-all | bytes 1048576 | tf_op jit(solution)/shard_map/all_to_all | solution.py:50
  77.0 0.1 chips_total.1
  77.1 15.8 %all_to_all.22.source_ref = bf16[64,32,128]{2,1,0:T(8,128)(2,1)S(1)} all-to-all(bf16[64,32,128]{2,1,0:T(8,128)(2,1)S(1)} %chips_total.1), channel_id=1, replica_groups=mesh['vocab_0'=4,'vocab_1'=4,'vocab_2'=2,'dp'=4] {'vocab_0','vocab_1','dp'}, dimensions={0} | all-to-all | bytes 1048576 | tf_op jit(solution)/shard_map/all_to_all | solution.py:50
  93.0 0.0 copy-start
  93.0 2.9 %collective-permute-start.1 = (bf16[64,32,128]{2,1,0:T(8,128)(2,1)S(1)}, bf16[64,32,128]{2,1,0:T(8,128)(2,1)S(1)}, u32[]{:S(2)}, u32[]{:S(2)}) collective-permute-start(bf16[64,32,128]{2,1,0:T(8,128)(2,1)S(1)} %all_to_all.22.source_ref), channel_id=1, source_target_pairs={{0,4},{4,0},{1,5},{5,1},{2,6},{6,2},{3,7},{7,3},{8,12},{12,8},{9,1... | collective-permute-start | bytes 1572872 | tf_op jit(solution)/shard_map/ppermute | solution.py:512
  95.8 7.8 %rows_sum.1 = f32[8192,128]{1,0:T(8,128)} custom-call(s32[128,1,16]{2,1,0:T(1,128)S(1)} %all-to-all-done.index_ref, bf16[128,32,128]{2,1,0:T(8,128)(2,1)S(1)} %all_to_all.20.rows_ref.grads_ref), custom_call_target="tpu_custom_call" | custom-call | flops 268435456 | bytes 6291456 | tf_op jit(solution)/shard_map/rows_sum/pallas_call | solution.py:260
  103.7 0.0 copy-done
  103.7 4.9 %hidden_rows.1 = bf16[1024,4096]{1,0:T(8,128)(2,1)} custom-call(bf16[128,1024]{1,0:T(8,128)(2,1)S(1)} %get-tuple-element.13.emb_ref, bf16[128,4096]{1,0:T(8,128)(2,1)S(1)} %copy-done), custom_call_target="tpu_custom_call" | custom-call | flops 1073741824 | bytes 9437184 | tf_op jit(solution)/shard_map/hidden_rows/pallas_call | solution.py:474
  108.6 1.0 own_result.1.rest_0_
  109.6 0.0 collective-permute-done.1.source_ref
  109.6 1.0 result.1
Async XLA Ops:
  1.3 0.7 copy-start.1
  4.0 21.1 %all-to-all-start = ((s32[128,1,16]{2,1,0:T(1,128)}), s32[128,1,16]{2,1,0:T(1,128)S(1)}, u32[]{:S(2)}, u32[]{:S(2)}) async-start(s32[128,1,16]{2,1,0:T(1,128)} %bitcast.2), calls=%async_computation | async-start | bytes 131072 | tf_op jit(solution)/shard_map/all_to_all | solution.py:50
  56.7 3.0 %collective-permute-start = (f32[128,2048]{1,0:T(8,128)S(1)}, f32[128,2048]{1,0:T(8,128)S(1)}, u32[]{:S(2)}, u32[]{:S(2)}) collective-permute-start(f32[128,2048]{1,0:T(8,128)S(1)} %get-tuple-element.14), channel_id=1, source_target_pairs={{0,4},{4,0},{1,5},{5,1},{2,6},{6,2},{3,7},{7,3},{8,12},{12,8},{9,1... | collective-permute-start | bytes 3145736 | tf_op jit(solution)/shard_map/ppermute | solution.py:505
  93.0 10.7 %copy-start = (bf16[128,4096]{1,0:T(8,128)(2,1)S(1)}, bf16[128,4096]{1,0:T(8,128)(2,1)}, u32[]{:S(2)}) copy-start(bf16[128,4096]{1,0:T(8,128)(2,1)} %proj_ref.1) | copy-start | bytes 3145732
  93.0 16.6 %collective-permute-start.1 = (bf16[64,32,128]{2,1,0:T(8,128)(2,1)S(1)}, bf16[64,32,128]{2,1,0:T(8,128)(2,1)S(1)}, u32[]{:S(2)}, u32[]{:S(2)}) collective-permute-start(bf16[64,32,128]{2,1,0:T(8,128)(2,1)S(1)} %all_to_all.22.source_ref), channel_id=1, source_target_pairs={{0,4},{4,0},{1,5},{5,1},{2,6},{6,2},{3,7},{7,3},{8,12},{12,8},{9,1... | collective-permute-start | bytes 1572872 | tf_op jit(solution)/shard_map/ppermute | solution.py:512

commit v3 on v2

--- a/solution.py
+++ b/solution.py
@@ -50,38 +50,40 @@
     return lax.all_to_all(blocks, axes, split_axis=0, concat_axis=0, tiled=True)
 
 
-def prepare_kernel(shift, capacity, core_ref, count_ref, ids_ref, slot_ref, request_ref):
+def prepare_kernel(
+    shift, capacity, core_ref, count_ref, ids_ref, slot_ref, request_ref, hits_ref, row_ref
+):
     del core_ref, count_ref
     n = request_ref.shape[0]
     chunks, lanes = ids_ref.shape
     holder = lax.broadcasted_iota(jnp.int32, (n, lanes), 0)
-    before = one_hot(
-        lax.broadcasted_iota(jnp.int32, (lanes, lanes), 0)
-        < lax.broadcasted_iota(jnp.int32, (lanes, lanes), 1)
-    )
+    line = lax.broadcasted_iota(jnp.int32, (lanes, 2 * lanes), 0)
+    column = lax.broadcasted_iota(jnp.int32, (lanes, 2 * lanes), 1)
+    before = one_hot(line < column)
     place = lax.broadcasted_iota(jnp.int32, (capacity, lanes), 0)
-    seen = jnp.zeros((n, 1), F32)
-    high = jnp.zeros((n, capacity), F32)
-    low = jnp.zeros((n, capacity), F32)
+    seen = jnp.zeros((n, lanes), F32)
     ids = ids_ref[...]
     owner = lax.shift_right_logical(ids, shift)
     row = ids & ((1 << shift) - 1)
+    upper = lax.shift_right_logical(row, 7).astype(F32)
+    lower = (row & 127).astype(F32)
     for k in range(chunks):
         own = owner[k : k + 1, :]
         hit = holder == own
-        hits = one_hot(hit)
-        earlier = dot(hits, before) + seen
+        columns = slice(k * lanes, (k + 1) * lanes)
+        hits_ref[:, columns] = one_hot(hit)
+        counted = dot(hits_ref[:, columns], before)
+        earlier = counted[:, :lanes] + seen
+        seen = seen + counted[:, lanes:]
         rank = jnp.sum(jnp.where(hit, earlier, 0.0), axis=0, keepdims=True).astype(jnp.int32)
-        seen = seen + jnp.sum(jnp.where(hit, 1.0, 0.0), axis=1, keepdims=True)
         per = slot_ref.shape[2] // lanes
         slot_ref[k // per, :, (k % per) * lanes : (k % per + 1) * lanes] = own * capacity + rank
         mine = place == rank
-        line = row[k : k + 1, :]
-        upper = lax.shift_right_logical(line, 7).astype(F32)
-        lower = (line & 127).astype(F32)
-        high = high + dot(hits, jnp.where(mine, upper, 0.0).astype(BF16), ((1,), (1,)))
-        low = low + dot(hits, jnp.where(mine, lower, 0.0).astype(BF16), ((1,), (1,)))
-    request_ref[...] = (high * 128.0 + low).astype(jnp.int32)
+        high = jnp.where(mine, upper[k : k + 1, :], 0.0)
+        low = jnp.where(mine, lower[k : k + 1, :], 0.0)
+        row_ref[:, columns] = jnp.concatenate([high, low], axis=0).astype(BF16)
+    split = dot(hits_ref[...], row_ref[...], ((1,), (1,)))
+    request_ref[...] = (split[:, :capacity] * 128.0 + split[:, capacity:]).astype(jnp.int32)
 
 
 def prepare(core, counts, token_ids, held_rows, n, capacity, block):
@@ -96,6 +98,10 @@
         ),
         in_specs=[SMEM, SMEM, VMEM],
         out_specs=(VMEM, VMEM),
+        scratch_shapes=[
+            pltpu.VMEM((n, tokens), BF16),
+            pltpu.VMEM((2 * capacity, tokens), BF16),
+        ],
         compiler_params=params(8),
         cost_estimate=cost(1 << 26, 1 << 16),
         name="prepare",
@@ -158,10 +164,11 @@
     )(counts, slots, in_hbm(projection), in_hbm(cotangent), in_hbm(table))
 
 
-def pick_kernel(index_ref, grads_ref, held_ref, out_ref, index, table, stage, sem):
-    copy = pltpu.make_async_copy(index_ref, index, sem)
+def pick_kernel(index_ref, grads_ref, held_ref, out_ref, index, packed, table, stage, sem):
+    n, _, capacity = index_ref.shape
+    packed[...] = index_ref[...].reshape(n, capacity).T
+    copy = pltpu.make_async_copy(packed, index, sem)
     copy.start()
-    n, _, capacity = index_ref.shape
     for p in range(n):
         out_ref[p, capacity:, :] = grads_ref[p * capacity : (p + 1) * capacity, :]
     step = 256
@@ -172,14 +179,14 @@
         table[rows, :] = held_ref[rows, :].astype(F32)
 
     copy.wait()
-    unroll = 4
+    unroll = 8
 
     @pl.loop(0, n // unroll)
     def _(q):
         for k in range(unroll):
             p = q * unroll + k
             for r in range(capacity):
-                stage[pl.ds(p * capacity + r, 1), :] = table[pl.ds(index[p, 0, r], 1), :]
+                stage[pl.ds(p * capacity + r, 1), :] = table[pl.ds(index[r, p], 1), :]
 
     for p in range(n):
         out_ref[p, :capacity, :] = stage[p * capacity : (p + 1) * capacity, :].astype(BF16)
@@ -195,7 +202,8 @@
         in_specs=[VMEM, VMEM, VMEM],
         out_specs=VMEM,
         scratch_shapes=[
-            pltpu.SMEM(received.shape, jnp.int32),
+            pltpu.SMEM((capacity, n), jnp.int32),
+            pltpu.VMEM((capacity, n), jnp.int32),
             pltpu.VMEM((rows, width), F32),
             pltpu.VMEM((slots, width), F32),
             pltpu.SemaphoreType.DMA(()),
@@ -374,15 +382,24 @@
     )(core, embedded, in_hbm(cotangent))
 
 
-def parts_kernel(tiles, mine_ref, other_ref, out_ref):
+def parts_kernel(tiles, mine_ref, other_ref, out_hbm, parts, sems):
     groups = mine_ref.shape[1] // (tiles * LANES)
-    for g in range(mine_ref.shape[0] // 8):
-        rows = slice(8 * g, 8 * g + 8)
-        for j in range(groups):
-            columns = slice(j * tiles * LANES, (j + 1) * tiles * LANES)
-            total = mine_ref[rows, columns] + other_ref[rows, columns]
-            block = [total[:, t * LANES : (t + 1) * LANES] for t in range(tiles)]
-            out_ref[g * groups + j] = jnp.concatenate(block, axis=0).astype(BF16)
+    steps = sems.shape[0]
+    per = mine_ref.shape[0] // 8 // steps
+    copies = []
+    for i in range(steps):
+        for g in range(i * per, (i + 1) * per):
+            rows = slice(8 * g, 8 * g + 8)
+            for j in range(groups):
+                columns = slice(j * tiles * LANES, (j + 1) * tiles * LANES)
+                total = mine_ref[rows, columns] + other_ref[rows, columns]
+                block = [total[:, t * LANES : (t + 1) * LANES] for t in range(tiles)]
+                parts[g * groups + j] = jnp.concatenate(block, axis=0).astype(BF16)
+        chips = pl.ds(i * per * groups, per * groups)
+        copies.append(pltpu.make_async_copy(parts.at[chips], out_hbm.at[chips], sems.at[i]))
+        copies[-1].start()
+    for copy in copies:
+        copy.wait()
 
 
 def chip_parts(mine, other, chips):
@@ -392,7 +409,11 @@
         functools.partial(parts_kernel, tiles),
         out_shape=jax.ShapeDtypeStruct((chips, 8 * tiles, LANES), BF16),
         in_specs=[VMEM, VMEM],
-        out_specs=VMEM,
+        out_specs=HBM,
+        scratch_shapes=[
+            pltpu.VMEM((chips, 8 * tiles, LANES), BF16),
+            pltpu.SemaphoreType.DMA((4,)),
+        ],
         compiler_params=params(8),
         cost_estimate=cost(1 << 24, 3 << 20),
         name="chip_parts",

time: 111 us -> 111 us (level)
  no operation moved by 1% of the time
where the time goes in v3:
time: 111 us; the launch traced here: 110 us
  blocking collectives  58.2 us (52%)
  Pallas kernels  31.4 us (28%)
  starting transfers between devices  14.9 us (13%)
  waiting for transfers between devices  3.65 us (3%)
  between operations  1.38 us (1%)
    all_to_all x3, blocking collectives, exchange(): return lax.all_to_all(blocks, axes, split_axis=0, concat_axis=0, tiled=True)  58.2 us
    all_to_all x1, starting transfers between devices, exchange(): return lax.all_to_all(blocks, axes, split_axis=0, concat_axis=0, tiled=True)  11.5 us
    pallas_call x1, Pallas kernels, rows_sum(): pl.pallas_call(rows_sum_kernel, out_shape=jax.ShapeDtypeStruct((held_rows...  7.8 us
    pallas_call x1, Pallas kernels, placed_grads(): pl.pallas_call(grads_kernel, out_shape=(jax.ShapeDtypeStruct((n_slots, wi...  5.94 us
    pallas_call x1, Pallas kernels, hidden_rows(): pl.pallas_call(hidden_kernel, grid=(tokens // block,), out_shape=jax.Shap...  4.89 us
    all_to_all x1, waiting for transfers between devices, exchange(): return lax.all_to_all(blocks, axes, split_axis=0, concat_axis=0, tiled=True)  3.65 us
    pallas_call x1, Pallas kernels, picked_rows(): pl.pallas_call(pick_kernel, out_shape=jax.ShapeDtypeStruct((n, 2 * capaci...  3.11 us
    pallas_call x1, Pallas kernels, first_terms(): pl.pallas_call(first_terms_kernel, in_specs=[SMEM, SMEM, VMEM, VMEM, HBM]...  2.97 us
  transfers between devices with their start and end apart: 3, of which 1 were waited for; matrix products, arithmetic and copies ran while one was open for 0% of the time, Pallas kernels for 20%

profile of v3, /device:TPU:1, one launch (start us, length us, event | category | flops | bytes accessed | tf_op | source)
XLA Modules:
  0.0 110.2 jit_solution(17620195457660447785)
XLA Ops:
  1.3 0.0 copy-start.1
  1.3 0.7 copy-done.1
  2.0 1.2 %prepare.1 = (s32[4,1,256]{2,1,0:T(1,128)S(1)}, s32[128,16]{1,0:T(8,128)}) custom-call(s32[1]{0:T(128)} %bitcast.core_ref, s32[1]{0:T(128)S(6)} %copy.10.count_ref, s32[8,128]{1,0:T(8,128)S(1)} %bitcast.3), custom_call_target="tpu_custom_call" | custom-call | flops 67108864 | bytes 65536 | tf_op jit(solution)/shard_map/prepare/pallas_call | solution.py:93
  3.2 11.5 %all-to-all-start = ((s32[128,1,16]{2,1,0:T(1,128)}), s32[128,1,16]{2,1,0:T(1,128)S(1)}, u32[]{:S(2)}, u32[]{:S(2)}) async-start(s32[128,1,16]{2,1,0:T(1,128)} %bitcast.2), calls=%async_computation | async-start | bytes 131072 | tf_op jit(solution)/shard_map/all_to_all | solution.py:50
  14.7 5.9 %placed_grads.1 = (bf16[2048,128]{1,0:T(8,128)(2,1)S(1)}, bf16[8192,128]{1,0:T(8,128)(2,1)S(1)}) custom-call(s32[1]{0:T(128)S(6)} %copy.10.count_ref, s32[4,1,256]{2,1,0:T(1,128)S(1)} %get-tuple-element.9.slot_ref, bf16[128,4096]{1,0:T(8,128)(2,1)} %proj_ref.1, bf16[1024,4096]{1,0:T(8,128)(2,1)} %cot_hbm.5, bf16[8192,128]{1,0:T(8,128)(2,1)} %table_hbm.1), custom_call_target="tpu_custom_call" | custom-call | flops 1610612736 | bytes 10485760 | tf_op jit(solution)/shard_map/placed_grads/pallas_call | solution.py:146
  20.6 3.6 %all-to-all-done.index_ref = s32[128,1,16]{2,1,0:T(1,128)S(1)} async-done(((s32[128,1,16]{2,1,0:T(1,128)}), s32[128,1,16]{2,1,0:T(1,128)S(1)}, u32[]{:S(2)}, u32[]{:S(2)}) %all-to-all-start) | async-done | bytes 8224 | tf_op jit(solution)/shard_map/all_to_all | solution.py:50
  24.3 3.1 %picked_rows.1 = bf16[128,32,128]{2,1,0:T(8,128)(2,1)S(1)} custom-call(s32[128,1,16]{2,1,0:T(1,128)S(1)} %all-to-all-done.index_ref, bf16[2048,128]{1,0:T(8,128)(2,1)S(1)} %get-tuple-element.11.grads_ref, bf16[8192,128]{1,0:T(8,128)(2,1)S(1)} %get-tuple-element.12.held_ref), custom_call_target="tpu_custom_call" | custom-call | flops 67108864 | bytes 3145728 | tf_op jit(solution)/shard_map/picked_rows/pallas_call | solution.py:199
  27.4 25.2 %all_to_all.20.rows_ref.grads_ref = bf16[128,32,128]{2,1,0:T(8,128)(2,1)S(1)} all-to-all(bf16[128,32,128]{2,1,0:T(8,128)(2,1)S(1)} %picked_rows.1), channel_id=1, replica_groups=mesh['vocab_0'=4,'vocab_1'=4,'vocab_2'=2,'dp'=4] {'vocab_0','vocab_1','v..., dimensions={0} | all-to-all | bytes 2097152 | tf_op jit(solution)/shard_map/all_to_all | solution.py:50
  52.6 3.0 %first_terms.1 = (bf16[128,1024]{1,0:T(8,128)(2,1)S(1)}, f32[128,2048]{1,0:T(8,128)S(1)}) custom-call(s32[1]{0:T(128)} %bitcast.core_ref, s32[1]{0:T(128)S(6)} %copy.10.count_ref, s32[4,1,256]{2,1,0:T(1,128)S(1)} %get-tuple-element.9.slot_ref, bf16[128,32,128]{2,1,0:T(8,128)(2,1)S(1)} %all_to_all.20.rows_ref.grads_ref, bf16[1024,4096]{1,0:T(8,128)(2,1)} %cot_hbm.5), custom_call_target="tpu_custom_call" | custom-call | flops 805306368 | bytes 6291456 | tf_op jit(solution)/shard_map/first_terms/pallas_call | solution.py:349
  55.6 0.5 collective-permute-start
  56.1 2.5 %half_terms.1.mine_ref = f32[128,2048]{1,0:T(8,128)S(1)} custom-call(s32[1]{0:T(128)} %bitcast.core_ref, bf16[128,1024]{1,0:T(8,128)(2,1)S(1)} %get-tuple-element.13.emb_ref, bf16[1024,4096]{1,0:T(8,128)(2,1)} %cot_hbm.5), custom_call_target="tpu_custom_call" | custom-call | flops 536870912 | bytes 5242880 | tf_op jit(solution)/shard_map/half_terms/pallas_call | solution.py:370
  58.6 0.0 collective-permute-done.other_ref
  58.6 0.8 chip_parts.1
  59.5 17.2 %all_to_all.21.parts_ref = bf16[64,32,128]{2,1,0:T(8,128)(2,1)S(1)} all-to-all(bf16[64,32,128]{2,1,0:T(8,128)(2,1)S(1)} %chip_parts.1), channel_id=1, replica_groups=mesh['vocab_0'=4,'vocab_1'=4,'vocab_2'=2,'dp'=4] {'vocab_0','vocab_1','dp'}, dimensions={0} | all-to-all | bytes 1048576 | tf_op jit(solution)/shard_map/all_to_all | solution.py:50
  76.6 0.1 chips_total.1
  76.8 15.8 %all_to_all.22.source_ref = bf16[64,32,128]{2,1,0:T(8,128)(2,1)S(1)} all-to-all(bf16[64,32,128]{2,1,0:T(8,128)(2,1)S(1)} %chips_total.1), channel_id=1, replica_groups=mesh['vocab_0'=4,'vocab_1'=4,'vocab_2'=2,'dp'=4] {'vocab_0','vocab_1','dp'}, dimensions={0} | all-to-all | bytes 1048576 | tf_op jit(solution)/shard_map/all_to_all | solution.py:50
  92.6 0.0 copy-start
  92.6 2.9 %collective-permute-start.1 = (bf16[64,32,128]{2,1,0:T(8,128)(2,1)S(1)}, bf16[64,32,128]{2,1,0:T(8,128)(2,1)S(1)}, u32[]{:S(2)}, u32[]{:S(2)}) collective-permute-start(bf16[64,32,128]{2,1,0:T(8,128)(2,1)S(1)} %all_to_all.22.source_ref), channel_id=1, source_target_pairs={{0,4},{4,0},{1,5},{5,1},{2,6},{6,2},{3,7},{7,3},{8,12},{12,8},{9,1... | collective-permute-start | bytes 1572872 | tf_op jit(solution)/shard_map/ppermute | solution.py:533
  95.5 7.8 %rows_sum.1 = f32[8192,128]{1,0:T(8,128)} custom-call(s32[128,1,16]{2,1,0:T(1,128)S(1)} %all-to-all-done.index_ref, bf16[128,32,128]{2,1,0:T(8,128)(2,1)S(1)} %all_to_all.20.rows_ref.grads_ref), custom_call_target="tpu_custom_call" | custom-call | flops 268435456 | bytes 6291456 | tf_op jit(solution)/shard_map/rows_sum/pallas_call | solution.py:268
  103.3 0.0 copy-done
  103.3 4.9 %hidden_rows.1 = bf16[1024,4096]{1,0:T(8,128)(2,1)} custom-call(bf16[128,1024]{1,0:T(8,128)(2,1)S(1)} %get-tuple-element.13.emb_ref, bf16[128,4096]{1,0:T(8,128)(2,1)S(1)} %copy-done), custom_call_target="tpu_custom_call" | custom-call | flops 1073741824 | bytes 9437184 | tf_op jit(solution)/shard_map/hidden_rows/pallas_call | solution.py:495
  108.2 1.0 own_result.1.rest_0_
  109.2 0.0 collective-permute-done.1.source_ref
  109.2 1.0 result.1
Async XLA Ops:
  1.3 0.7 copy-start.1
  3.2 21.1 %all-to-all-start = ((s32[128,1,16]{2,1,0:T(1,128)}), s32[128,1,16]{2,1,0:T(1,128)S(1)}, u32[]{:S(2)}, u32[]{:S(2)}) async-start(s32[128,1,16]{2,1,0:T(1,128)} %bitcast.2), calls=%async_computation | async-start | bytes 131072 | tf_op jit(solution)/shard_map/all_to_all | solution.py:50
  55.6 3.0 %collective-permute-start = (f32[128,2048]{1,0:T(8,128)S(1)}, f32[128,2048]{1,0:T(8,128)S(1)}, u32[]{:S(2)}, u32[]{:S(2)}) collective-permute-start(f32[128,2048]{1,0:T(8,128)S(1)} %get-tuple-element.14), channel_id=1, source_target_pairs={{0,4},{4,0},{1,5},{5,1},{2,6},{6,2},{3,7},{7,3},{8,12},{12,8},{9,1... | collective-permute-start | bytes 3145736 | tf_op jit(solution)/shard_map/ppermute | solution.py:526
  92.6 10.7 %copy-start = (bf16[128,4096]{1,0:T(8,128)(2,1)S(1)}, bf16[128,4096]{1,0:T(8,128)(2,1)}, u32[]{:S(2)}) copy-start(bf16[128,4096]{1,0:T(8,128)(2,1)} %proj_ref.1) | copy-start | bytes 3145732
  92.6 16.6 %collective-permute-start.1 = (bf16[64,32,128]{2,1,0:T(8,128)(2,1)S(1)}, bf16[64,32,128]{2,1,0:T(8,128)(2,1)S(1)}, u32[]{:S(2)}, u32[]{:S(2)}) collective-permute-start(bf16[64,32,128]{2,1,0:T(8,128)(2,1)S(1)} %all_to_all.22.source_ref), channel_id=1, source_target_pairs={{0,4},{4,0},{1,5},{5,1},{2,6},{6,2},{3,7},{7,3},{8,12},{12,8},{9,1... | collective-permute-start | bytes 1572872 | tf_op jit(solution)/shard_map/ppermute | solution.py:533

commit v4 on v3

--- a/solution.py
+++ b/solution.py
@@ -420,13 +420,19 @@
     )(mine, other)
 
 
-def total_kernel(parts_ref, out_ref):
+def total_kernel(parts_ref, out_hbm, total_ref, sems):
     total = parts_ref[0].astype(F32)
     for p in range(1, parts_ref.shape[0]):
         total += parts_ref[p].astype(F32)
-    total = total.astype(BF16)
-    for p in range(out_ref.shape[0]):
-        out_ref[p] = total
+    total_ref[...] = total.astype(BF16)
+    copies = [
+        pltpu.make_async_copy(total_ref, out_hbm.at[p], sems.at[p])
+        for p in range(out_hbm.shape[0])
+    ]
+    for copy in copies:
+        copy.start()
+    for copy in copies:
+        copy.wait()
 
 
 def chips_total(parts):
@@ -434,7 +440,11 @@
         total_kernel,
         out_shape=jax.ShapeDtypeStruct(parts.shape, BF16),
         in_specs=[VMEM],
-        out_specs=VMEM,
+        out_specs=HBM,
+        scratch_shapes=[
+            pltpu.VMEM(parts.shape[1:], BF16),
+            pltpu.SemaphoreType.DMA((parts.shape[0],)),
+        ],
         compiler_params=params(8),
         cost_estimate=cost(1 << 24, 1 << 20),
         name="chips_total",

time: 111 us -> 112 us (level)
  Pallas kernels: 31.4 us -> 32.8 us
    pallas_call x1, Pallas kernels: 0.11 us -> 1.46 us  [chips_total(): pl.pallas_call(total_kernel, out_shape=jax.ShapeDtypeStruct(parts.shape,...]
where the time goes in v4:
time: 112 us
  blocking collectives  58.2 us (52%)
  Pallas kernels  32.8 us (29%)
  starting transfers between devices  14.9 us (13%)
  waiting for transfers between devices  3.65 us (3%)
  between operations  1.39 us (1%)
    all_to_all x3, blocking collectives, exchange(): return lax.all_to_all(blocks, axes, split_axis=0, concat_axis=0, tiled=True)  58.2 us
    all_to_all x1, starting transfers between devices, exchange(): return lax.all_to_all(blocks, axes, split_axis=0, concat_axis=0, tiled=True)  11.5 us
    pallas_call x1, Pallas kernels, rows_sum(): pl.pallas_call(rows_sum_kernel, out_shape=jax.ShapeDtypeStruct((held_rows...  7.8 us
    pallas_call x1, Pallas kernels, placed_grads(): pl.pallas_call(grads_kernel, out_shape=(jax.ShapeDtypeStruct((n_slots, wi...  5.94 us
    pallas_call x1, Pallas kernels, hidden_rows(): pl.pallas_call(hidden_kernel, grid=(tokens // block,), out_shape=jax.Shap...  4.89 us
    all_to_all x1, waiting for transfers between devices, exchange(): return lax.all_to_all(blocks, axes, split_axis=0, concat_axis=0, tiled=True)  3.65 us
    pallas_call x1, Pallas kernels, picked_rows(): pl.pallas_call(pick_kernel, out_shape=jax.ShapeDtypeStruct((n, 2 * capaci...  3.11 us
    pallas_call x1, Pallas kernels, first_terms(): pl.pallas_call(first_terms_kernel, in_specs=[SMEM, SMEM, VMEM, VMEM, HBM]...  2.97 us
  transfers between devices with their start and end apart: 3, of which 1 were waited for; matrix products, arithmetic and copies ran while one was open for 0% of the time, Pallas kernels for 20%

profile of v4, /device:TPU:1, one launch (start us, length us, event | category | flops | bytes accessed | tf_op | source)
XLA Modules:
  0.0 111.6 jit_solution(14794764389043206561)
XLA Ops:
  1.3 0.0 copy-start.1
  1.3 0.7 copy-done.1
  2.0 1.2 %prepare.1 = (s32[4,1,256]{2,1,0:T(1,128)S(1)}, s32[128,16]{1,0:T(8,128)}) custom-call(s32[1]{0:T(128)} %bitcast.core_ref, s32[1]{0:T(128)S(6)} %copy.10.count_ref, s32[8,128]{1,0:T(8,128)S(1)} %bitcast.3), custom_call_target="tpu_custom_call" | custom-call | flops 67108864 | bytes 65536 | tf_op jit(solution)/shard_map/prepare/pallas_call | solution.py:93
  3.2 11.5 %all-to-all-start = ((s32[128,1,16]{2,1,0:T(1,128)}), s32[128,1,16]{2,1,0:T(1,128)S(1)}, u32[]{:S(2)}, u32[]{:S(2)}) async-start(s32[128,1,16]{2,1,0:T(1,128)} %bitcast.2), calls=%async_computation | async-start | bytes 131072 | tf_op jit(solution)/shard_map/all_to_all | solution.py:50
  14.7 5.9 %placed_grads.1 = (bf16[2048,128]{1,0:T(8,128)(2,1)S(1)}, bf16[8192,128]{1,0:T(8,128)(2,1)S(1)}) custom-call(s32[1]{0:T(128)S(6)} %copy.10.count_ref, s32[4,1,256]{2,1,0:T(1,128)S(1)} %get-tuple-element.9.slot_ref, bf16[128,4096]{1,0:T(8,128)(2,1)} %proj_ref.1, bf16[1024,4096]{1,0:T(8,128)(2,1)} %cot_hbm.5, bf16[8192,128]{1,0:T(8,128)(2,1)} %table_hbm.1), custom_call_target="tpu_custom_call" | custom-call | flops 1610612736 | bytes 10485760 | tf_op jit(solution)/shard_map/placed_grads/pallas_call | solution.py:146
  20.6 3.6 %all-to-all-done.index_ref = s32[128,1,16]{2,1,0:T(1,128)S(1)} async-done(((s32[128,1,16]{2,1,0:T(1,128)}), s32[128,1,16]{2,1,0:T(1,128)S(1)}, u32[]{:S(2)}, u32[]{:S(2)}) %all-to-all-start) | async-done | bytes 8224 | tf_op jit(solution)/shard_map/all_to_all | solution.py:50
  24.3 3.1 %picked_rows.1 = bf16[128,32,128]{2,1,0:T(8,128)(2,1)S(1)} custom-call(s32[128,1,16]{2,1,0:T(1,128)S(1)} %all-to-all-done.index_ref, bf16[2048,128]{1,0:T(8,128)(2,1)S(1)} %get-tuple-element.11.grads_ref, bf16[8192,128]{1,0:T(8,128)(2,1)S(1)} %get-tuple-element.12.held_ref), custom_call_target="tpu_custom_call" | custom-call | flops 67108864 | bytes 3145728 | tf_op jit(solution)/shard_map/picked_rows/pallas_call | solution.py:199
  27.4 25.2 %all_to_all.20.rows_ref.grads_ref = bf16[128,32,128]{2,1,0:T(8,128)(2,1)S(1)} all-to-all(bf16[128,32,128]{2,1,0:T(8,128)(2,1)S(1)} %picked_rows.1), channel_id=1, replica_groups=mesh['vocab_0'=4,'vocab_1'=4,'vocab_2'=2,'dp'=4] {'vocab_0','vocab_1','v..., dimensions={0} | all-to-all | bytes 2097152 | tf_op jit(solution)/shard_map/all_to_all | solution.py:50
  52.6 3.0 %first_terms.1 = (bf16[128,1024]{1,0:T(8,128)(2,1)S(1)}, f32[128,2048]{1,0:T(8,128)S(1)}) custom-call(s32[1]{0:T(128)} %bitcast.core_ref, s32[1]{0:T(128)S(6)} %copy.10.count_ref, s32[4,1,256]{2,1,0:T(1,128)S(1)} %get-tuple-element.9.slot_ref, bf16[128,32,128]{2,1,0:T(8,128)(2,1)S(1)} %all_to_all.20.rows_ref.grads_ref, bf16[1024,4096]{1,0:T(8,128)(2,1)} %cot_hbm.5), custom_call_target="tpu_custom_call" | custom-call | flops 805306368 | bytes 6291456 | tf_op jit(solution)/shard_map/first_terms/pallas_call | solution.py:349
  55.6 0.5 collective-permute-start
  56.1 2.5 %half_terms.1.mine_ref = f32[128,2048]{1,0:T(8,128)S(1)} custom-call(s32[1]{0:T(128)} %bitcast.core_ref, bf16[128,1024]{1,0:T(8,128)(2,1)S(1)} %get-tuple-element.13.emb_ref, bf16[1024,4096]{1,0:T(8,128)(2,1)} %cot_hbm.5), custom_call_target="tpu_custom_call" | custom-call | flops 536870912 | bytes 5242880 | tf_op jit(solution)/shard_map/half_terms/pallas_call | solution.py:370
  58.6 0.0 collective-permute-done.other_ref
  58.6 0.8 chip_parts.1
  59.5 17.2 %all_to_all.21.parts_ref = bf16[64,32,128]{2,1,0:T(8,128)(2,1)S(1)} all-to-all(bf16[64,32,128]{2,1,0:T(8,128)(2,1)S(1)} %chip_parts.1), channel_id=1, replica_groups=mesh['vocab_0'=4,'vocab_1'=4,'vocab_2'=2,'dp'=4] {'vocab_0','vocab_1','dp'}, dimensions={0} | all-to-all | bytes 1048576 | tf_op jit(solution)/shard_map/all_to_all | solution.py:50
  76.6 1.5 %chips_total.1 = bf16[64,32,128]{2,1,0:T(8,128)(2,1)S(1)} custom-call(bf16[64,32,128]{2,1,0:T(8,128)(2,1)S(1)} %all_to_all.21.parts_ref), custom_call_target="tpu_custom_call" | custom-call | flops 16777216 | bytes 1048576 | tf_op jit(solution)/shard_map/chips_total/pallas_call | solution.py:439
  78.1 15.8 %all_to_all.22.source_ref = bf16[64,32,128]{2,1,0:T(8,128)(2,1)S(1)} all-to-all(bf16[64,32,128]{2,1,0:T(8,128)(2,1)S(1)} %chips_total.1), channel_id=1, replica_groups=mesh['vocab_0'=4,'vocab_1'=4,'vocab_2'=2,'dp'=4] {'vocab_0','vocab_1','dp'}, dimensions={0} | all-to-all | bytes 1048576 | tf_op jit(solution)/shard_map/all_to_all | solution.py:50
  93.9 0.0 copy-start
  93.9 2.9 %collective-permute-start.1 = (bf16[64,32,128]{2,1,0:T(8,128)(2,1)S(1)}, bf16[64,32,128]{2,1,0:T(8,128)(2,1)S(1)}, u32[]{:S(2)}, u32[]{:S(2)}) collective-permute-start(bf16[64,32,128]{2,1,0:T(8,128)(2,1)S(1)} %all_to_all.22.source_ref), channel_id=1, source_target_pairs={{0,4},{4,0},{1,5},{5,1},{2,6},{6,2},{3,7},{7,3},{8,12},{12,8},{9,1... | collective-permute-start | bytes 1572872 | tf_op jit(solution)/shard_map/ppermute | solution.py:543
  96.8 7.8 %rows_sum.1 = f32[8192,128]{1,0:T(8,128)} custom-call(s32[128,1,16]{2,1,0:T(1,128)S(1)} %all-to-all-done.index_ref, bf16[128,32,128]{2,1,0:T(8,128)(2,1)S(1)} %all_to_all.20.rows_ref.grads_ref), custom_call_target="tpu_custom_call" | custom-call | flops 268435456 | bytes 6291456 | tf_op jit(solution)/shard_map/rows_sum/pallas_call | solution.py:268
  104.6 0.0 copy-done
  104.6 4.9 %hidden_rows.1 = bf16[1024,4096]{1,0:T(8,128)(2,1)} custom-call(bf16[128,1024]{1,0:T(8,128)(2,1)S(1)} %get-tuple-element.13.emb_ref, bf16[128,4096]{1,0:T(8,128)(2,1)S(1)} %copy-done), custom_call_target="tpu_custom_call" | custom-call | flops 1073741824 | bytes 9437184 | tf_op jit(solution)/shard_map/hidden_rows/pallas_call | solution.py:505
  109.5 1.0 own_result.1.rest_0_
  110.6 0.0 collective-permute-done.1.source_ref
  110.6 1.0 result.1
Async XLA Ops:
  1.3 0.7 copy-start.1
  3.2 21.1 %all-to-all-start = ((s32[128,1,16]{2,1,0:T(1,128)}), s32[128,1,16]{2,1,0:T(1,128)S(1)}, u32[]{:S(2)}, u32[]{:S(2)}) async-start(s32[128,1,16]{2,1,0:T(1,128)} %bitcast.2), calls=%async_computation | async-start | bytes 131072 | tf_op jit(solution)/shard_map/all_to_all | solution.py:50
  55.6 3.0 %collective-permute-start = (f32[128,2048]{1,0:T(8,128)S(1)}, f32[128,2048]{1,0:T(8,128)S(1)}, u32[]{:S(2)}, u32[]{:S(2)}) collective-permute-start(f32[128,2048]{1,0:T(8,128)S(1)} %get-tuple-element.14), channel_id=1, source_target_pairs={{0,4},{4,0},{1,5},{5,1},{2,6},{6,2},{3,7},{7,3},{8,12},{12,8},{9,1... | collective-permute-start | bytes 3145736 | tf_op jit(solution)/shard_map/ppermute | solution.py:536
  93.9 10.7 %copy-start = (bf16[128,4096]{1,0:T(8,128)(2,1)S(1)}, bf16[128,4096]{1,0:T(8,128)(2,1)}, u32[]{:S(2)}) copy-start(bf16[128,4096]{1,0:T(8,128)(2,1)} %proj_ref.1) | copy-start | bytes 3145732
  93.9 16.6 %collective-permute-start.1 = (bf16[64,32,128]{2,1,0:T(8,128)(2,1)S(1)}, bf16[64,32,128]{2,1,0:T(8,128)(2,1)S(1)}, u32[]{:S(2)}, u32[]{:S(2)}) collective-permute-start(bf16[64,32,128]{2,1,0:T(8,128)(2,1)S(1)} %all_to_all.22.source_ref), channel_id=1, source_target_pairs={{0,4},{4,0},{1,5},{5,1},{2,6},{6,2},{3,7},{7,3},{8,12},{12,8},{9,1... | collective-permute-start | bytes 1572872 | tf_op jit(solution)/shard_map/ppermute | solution.py:543

commit v5 on v4

--- a/solution.py
+++ b/solution.py
@@ -424,10 +424,13 @@
     total = parts_ref[0].astype(F32)
     for p in range(1, parts_ref.shape[0]):
         total += parts_ref[p].astype(F32)
-    total_ref[...] = total.astype(BF16)
+    total = total.astype(BF16)
+    several = total_ref.shape[0]
+    for p in range(several):
+        total_ref[p] = total
     copies = [
-        pltpu.make_async_copy(total_ref, out_hbm.at[p], sems.at[p])
-        for p in range(out_hbm.shape[0])
+        pltpu.make_async_copy(total_ref, out_hbm.at[pl.ds(i * several, several)], sems.at[i])
+        for i in range(out_hbm.shape[0] // several)
     ]
     for copy in copies:
         copy.start()
@@ -442,8 +445,8 @@
         in_specs=[VMEM],
         out_specs=HBM,
         scratch_shapes=[
-            pltpu.VMEM(parts.shape[1:], BF16),
-            pltpu.SemaphoreType.DMA((parts.shape[0],)),
+            pltpu.VMEM((parts.shape[0] // 4, *parts.shape[1:]), BF16),
+            pltpu.SemaphoreType.DMA((4,)),
         ],
         compiler_params=params(8),
         cost_estimate=cost(1 << 24, 1 << 20),

time: 112 us -> 111 us (level)
  no operation moved by 1% of the time
where the time goes in v5:
time: 111 us
  blocking collectives  58.2 us (52%)
  Pallas kernels  32.1 us (29%)
  starting transfers between devices  14.9 us (13%)
  waiting for transfers between devices  3.65 us (3%)
  between operations  1.39 us (1%)
    all_to_all x3, blocking collectives, exchange(): return lax.all_to_all(blocks, axes, split_axis=0, concat_axis=0, tiled=True)  58.2 us
    all_to_all x1, starting transfers between devices, exchange(): return lax.all_to_all(blocks, axes, split_axis=0, concat_axis=0, tiled=True)  11.5 us
    pallas_call x1, Pallas kernels, rows_sum(): pl.pallas_call(rows_sum_kernel, out_shape=jax.ShapeDtypeStruct((held_rows...  7.8 us
    pallas_call x1, Pallas kernels, placed_grads(): pl.pallas_call(grads_kernel, out_shape=(jax.ShapeDtypeStruct((n_slots, wi...  5.94 us
    pallas_call x1, Pallas kernels, hidden_rows(): pl.pallas_call(hidden_kernel, grid=(tokens // block,), out_shape=jax.Shap...  4.89 us
    all_to_all x1, waiting for transfers between devices, exchange(): return lax.all_to_all(blocks, axes, split_axis=0, concat_axis=0, tiled=True)  3.65 us
    pallas_call x1, Pallas kernels, picked_rows(): pl.pallas_call(pick_kernel, out_shape=jax.ShapeDtypeStruct((n, 2 * capaci...  3.11 us
    pallas_call x1, Pallas kernels, first_terms(): pl.pallas_call(first_terms_kernel, in_specs=[SMEM, SMEM, VMEM, VMEM, HBM]...  2.97 us
  transfers between devices with their start and end apart: 3, of which 1 were waited for; matrix products, arithmetic and copies ran while one was open for 0% of the time, Pallas kernels for 20%

profile of v5, /device:TPU:1, one launch (start us, length us, event | category | flops | bytes accessed | tf_op | source)
XLA Modules:
  0.0 110.9 jit_solution(10584382718259416557)
XLA Ops:
  1.3 0.0 copy-start.1
  1.3 0.7 copy-done.1
  2.0 1.2 %prepare.1 = (s32[4,1,256]{2,1,0:T(1,128)S(1)}, s32[128,16]{1,0:T(8,128)}) custom-call(s32[1]{0:T(128)} %bitcast.core_ref, s32[1]{0:T(128)S(6)} %copy.10.count_ref, s32[8,128]{1,0:T(8,128)S(1)} %bitcast.3), custom_call_target="tpu_custom_call" | custom-call | flops 67108864 | bytes 65536 | tf_op jit(solution)/shard_map/prepare/pallas_call | solution.py:93
  3.2 11.5 %all-to-all-start = ((s32[128,1,16]{2,1,0:T(1,128)}), s32[128,1,16]{2,1,0:T(1,128)S(1)}, u32[]{:S(2)}, u32[]{:S(2)}) async-start(s32[128,1,16]{2,1,0:T(1,128)} %bitcast.2), calls=%async_computation | async-start | bytes 131072 | tf_op jit(solution)/shard_map/all_to_all | solution.py:50
  14.7 5.9 %placed_grads.1 = (bf16[2048,128]{1,0:T(8,128)(2,1)S(1)}, bf16[8192,128]{1,0:T(8,128)(2,1)S(1)}) custom-call(s32[1]{0:T(128)S(6)} %copy.10.count_ref, s32[4,1,256]{2,1,0:T(1,128)S(1)} %get-tuple-element.9.slot_ref, bf16[128,4096]{1,0:T(8,128)(2,1)} %proj_ref.1, bf16[1024,4096]{1,0:T(8,128)(2,1)} %cot_hbm.5, bf16[8192,128]{1,0:T(8,128)(2,1)} %table_hbm.1), custom_call_target="tpu_custom_call" | custom-call | flops 1610612736 | bytes 10485760 | tf_op jit(solution)/shard_map/placed_grads/pallas_call | solution.py:146
  20.6 3.6 %all-to-all-done.index_ref = s32[128,1,16]{2,1,0:T(1,128)S(1)} async-done(((s32[128,1,16]{2,1,0:T(1,128)}), s32[128,1,16]{2,1,0:T(1,128)S(1)}, u32[]{:S(2)}, u32[]{:S(2)}) %all-to-all-start) | async-done | bytes 8224 | tf_op jit(solution)/shard_map/all_to_all | solution.py:50
  24.3 3.1 %picked_rows.1 = bf16[128,32,128]{2,1,0:T(8,128)(2,1)S(1)} custom-call(s32[128,1,16]{2,1,0:T(1,128)S(1)} %all-to-all-done.index_ref, bf16[2048,128]{1,0:T(8,128)(2,1)S(1)} %get-tuple-element.11.grads_ref, bf16[8192,128]{1,0:T(8,128)(2,1)S(1)} %get-tuple-element.12.held_ref), custom_call_target="tpu_custom_call" | custom-call | flops 67108864 | bytes 3145728 | tf_op jit(solution)/shard_map/picked_rows/pallas_call | solution.py:199
  27.4 25.2 %all_to_all.20.rows_ref.grads_ref = bf16[128,32,128]{2,1,0:T(8,128)(2,1)S(1)} all-to-all(bf16[128,32,128]{2,1,0:T(8,128)(2,1)S(1)} %picked_rows.1), channel_id=1, replica_groups=mesh['vocab_0'=4,'vocab_1'=4,'vocab_2'=2,'dp'=4] {'vocab_0','vocab_1','v..., dimensions={0} | all-to-all | bytes 2097152 | tf_op jit(solution)/shard_map/all_to_all | solution.py:50
  52.6 3.0 %first_terms.1 = (bf16[128,1024]{1,0:T(8,128)(2,1)S(1)}, f32[128,2048]{1,0:T(8,128)S(1)}) custom-call(s32[1]{0:T(128)} %bitcast.core_ref, s32[1]{0:T(128)S(6)} %copy.10.count_ref, s32[4,1,256]{2,1,0:T(1,128)S(1)} %get-tuple-element.9.slot_ref, bf16[128,32,128]{2,1,0:T(8,128)(2,1)S(1)} %all_to_all.20.rows_ref.grads_ref, bf16[1024,4096]{1,0:T(8,128)(2,1)} %cot_hbm.5), custom_call_target="tpu_custom_call" | custom-call | flops 805306368 | bytes 6291456 | tf_op jit(solution)/shard_map/first_terms/pallas_call | solution.py:349
  55.6 0.5 collective-permute-start
  56.1 2.5 %half_terms.1.mine_ref = f32[128,2048]{1,0:T(8,128)S(1)} custom-call(s32[1]{0:T(128)} %bitcast.core_ref, bf16[128,1024]{1,0:T(8,128)(2,1)S(1)} %get-tuple-element.13.emb_ref, bf16[1024,4096]{1,0:T(8,128)(2,1)} %cot_hbm.5), custom_call_target="tpu_custom_call" | custom-call | flops 536870912 | bytes 5242880 | tf_op jit(solution)/shard_map/half_terms/pallas_call | solution.py:370
  58.6 0.0 collective-permute-done.other_ref
  58.6 0.8 chip_parts.1
  59.5 17.2 %all_to_all.21.parts_ref = bf16[64,32,128]{2,1,0:T(8,128)(2,1)S(1)} all-to-all(bf16[64,32,128]{2,1,0:T(8,128)(2,1)S(1)} %chip_parts.1), channel_id=1, replica_groups=mesh['vocab_0'=4,'vocab_1'=4,'vocab_2'=2,'dp'=4] {'vocab_0','vocab_1','dp'}, dimensions={0} | all-to-all | bytes 1048576 | tf_op jit(solution)/shard_map/all_to_all | solution.py:50
  76.6 0.8 chips_total.1
  77.4 15.8 %all_to_all.22.source_ref = bf16[64,32,128]{2,1,0:T(8,128)(2,1)S(1)} all-to-all(bf16[64,32,128]{2,1,0:T(8,128)(2,1)S(1)} %chips_total.1), channel_id=1, replica_groups=mesh['vocab_0'=4,'vocab_1'=4,'vocab_2'=2,'dp'=4] {'vocab_0','vocab_1','dp'}, dimensions={0} | all-to-all | bytes 1048576 | tf_op jit(solution)/shard_map/all_to_all | solution.py:50
  93.3 0.0 copy-start
  93.3 2.9 %collective-permute-start.1 = (bf16[64,32,128]{2,1,0:T(8,128)(2,1)S(1)}, bf16[64,32,128]{2,1,0:T(8,128)(2,1)S(1)}, u32[]{:S(2)}, u32[]{:S(2)}) collective-permute-start(bf16[64,32,128]{2,1,0:T(8,128)(2,1)S(1)} %all_to_all.22.source_ref), channel_id=1, source_target_pairs={{0,4},{4,0},{1,5},{5,1},{2,6},{6,2},{3,7},{7,3},{8,12},{12,8},{9,1... | collective-permute-start | bytes 1572872 | tf_op jit(solution)/shard_map/ppermute | solution.py:546
  96.2 7.8 %rows_sum.1 = f32[8192,128]{1,0:T(8,128)} custom-call(s32[128,1,16]{2,1,0:T(1,128)S(1)} %all-to-all-done.index_ref, bf16[128,32,128]{2,1,0:T(8,128)(2,1)S(1)} %all_to_all.20.rows_ref.grads_ref), custom_call_target="tpu_custom_call" | custom-call | flops 268435456 | bytes 6291456 | tf_op jit(solution)/shard_map/rows_sum/pallas_call | solution.py:268
  104.0 0.0 copy-done
  104.0 4.9 %hidden_rows.1 = bf16[1024,4096]{1,0:T(8,128)(2,1)} custom-call(bf16[128,1024]{1,0:T(8,128)(2,1)S(1)} %get-tuple-element.13.emb_ref, bf16[128,4096]{1,0:T(8,128)(2,1)S(1)} %copy-done), custom_call_target="tpu_custom_call" | custom-call | flops 1073741824 | bytes 9437184 | tf_op jit(solution)/shard_map/hidden_rows/pallas_call | solution.py:508
  108.9 1.0 own_result.1.rest_0_
  109.9 0.0 collective-permute-done.1.source_ref
  109.9 1.0 result.1
Async XLA Ops:
  1.3 0.7 copy-start.1
  3.2 21.1 %all-to-all-start = ((s32[128,1,16]{2,1,0:T(1,128)}), s32[128,1,16]{2,1,0:T(1,128)S(1)}, u32[]{:S(2)}, u32[]{:S(2)}) async-start(s32[128,1,16]{2,1,0:T(1,128)} %bitcast.2), calls=%async_computation | async-start | bytes 131072 | tf_op jit(solution)/shard_map/all_to_all | solution.py:50
  55.6 3.0 %collective-permute-start = (f32[128,2048]{1,0:T(8,128)S(1)}, f32[128,2048]{1,0:T(8,128)S(1)}, u32[]{:S(2)}, u32[]{:S(2)}) collective-permute-start(f32[128,2048]{1,0:T(8,128)S(1)} %get-tuple-element.14), channel_id=1, source_target_pairs={{0,4},{4,0},{1,5},{5,1},{2,6},{6,2},{3,7},{7,3},{8,12},{12,8},{9,1... | collective-permute-start | bytes 3145736 | tf_op jit(solution)/shard_map/ppermute | solution.py:539
  93.3 10.7 %copy-start = (bf16[128,4096]{1,0:T(8,128)(2,1)S(1)}, bf16[128,4096]{1,0:T(8,128)(2,1)}, u32[]{:S(2)}) copy-start(bf16[128,4096]{1,0:T(8,128)(2,1)} %proj_ref.1) | copy-start | bytes 3145732
  93.3 16.6 %collective-permute-start.1 = (bf16[64,32,128]{2,1,0:T(8,128)(2,1)S(1)}, bf16[64,32,128]{2,1,0:T(8,128)(2,1)S(1)}, u32[]{:S(2)}, u32[]{:S(2)}) collective-permute-start(bf16[64,32,128]{2,1,0:T(8,128)(2,1)S(1)} %all_to_all.22.source_ref), channel_id=1, source_target_pairs={{0,4},{4,0},{1,5},{5,1},{2,6},{6,2},{3,7},{7,3},{8,12},{12,8},{9,1... | collective-permute-start | bytes 1572872 | tf_op jit(solution)/shard_map/ppermute | solution.py:546
